TPU v7x, 32 devices: a whole 2x2x4 slice. The times are simulated.
32 devices in a mesh: dp: 8 (over y, x, core), tensor: 4 (over z).
Axes of the slice: x: 2, y: 2, z: 4, core: 2. Of those that a mesh axis runs over, the one named last changes fastest.
Arguments:
- activations: bfloat16 [64, 1024, 1024], P(('dp', 'tensor')), may hold values from -6 to 6
- routes: int32 [64, 128], P('dp'), may hold values from 0 to 1023, as said below
- pic_start: int32 [64], P('dp'), may hold values from 0 to 768, as said below
- router_w: bfloat16 [1024], P('dp'), may hold values from -0.1875 to 0.1875
- gain_attn: bfloat16 [1024], P('dp'), may hold values from 0.099609375 to 1.8984375
- gain_mlp: bfloat16 [1024], P('dp'), may hold values from 0.099609375 to 1.8984375
- w_query: bfloat16 [1024, 1024], P('dp', 'tensor'), may hold values from -0.1875 to 0.1875
- w_key: bfloat16 [1024, 1024], P('dp', 'tensor'), may hold values from -0.1875 to 0.1875
- w_value: bfloat16 [1024, 1024], P('dp', 'tensor'), may hold values from -0.1875 to 0.1875
- w_proj: bfloat16 [1024, 1024], P('dp', 'tensor'), may hold values from -1.5 to 1.5
- w_up: bfloat16 [1024, 4096], P('dp', 'tensor'), may hold values from -0.1875 to 0.1875
- w_down: bfloat16 [1024, 4096], P('dp', 'tensor'), may hold values from -0.09375 to 0.09375
- cotangent: bfloat16 [64, 1024, 1024], P(('dp', 'tensor')), may hold values from -6 to 6
Outputs:
- result: bfloat16 [64, 1024, 1024], P(('dp', 'tensor'))
- grad_input: bfloat16 [64, 1024, 1024], P(('dp', 'tensor'))
- grad_router: float32 [1024], P('dp')
- grad_gain_attn: float32 [1024], P('dp')
- grad_gain_mlp: float32 [1024], P('dp')
- grad_query: float32 [1024, 1024], P('dp', 'tensor')
- grad_key: float32 [1024, 1024], P('dp', 'tensor')
- grad_value: float32 [1024, 1024], P('dp', 'tensor')
- grad_proj: float32 [1024, 1024], P('dp', 'tensor')
- grad_up: float32 [1024, 4096], P('dp', 'tensor')
- grad_down: float32 [1024, 4096], P('dp', 'tensor')
Inputs may be any that keep to these rules, and one draw needn't show every extreme that they name: `routes`: each row names 128 different positions of its sequence, in increasing order. A sequence's picture span holds the positions pic_start to pic_start + 255.
All inputs are finite; a program needn't handle non-finite values.
Results may differ from a plain program's by a relative error of at most 0.014.
Values may be sent and summed in bfloat16 or wider, within the bound.
A program may use at most 128 MiB of HBM per device.

v0:
```python
import math

import jax
import jax.numpy as jnp
from jax import lax
from jax.sharding import PartitionSpec as P

HD = 64
PIC = 256


inv_root_two = 0.7071067811865476
inv_root_two_pi = 0.3989422804014327


def normalize(values, gain):
    inverse = lax.rsqrt(jnp.mean(values * values, axis=-1, keepdims=True) + 1e-06)
    return (values * inverse * gain, inverse)


def norm_back(grad_out, values, inverse, gain):
    scaled = grad_out * gain
    grad_in = inverse * scaled - values * inverse * inverse * inverse * jnp.mean(
        scaled * values, axis=-1, keepdims=True
    )
    grad_gain = jnp.sum(grad_out * values * inverse, axis=(0, 1))
    return (grad_in, grad_gain)


def gelu_exact(values):
    return 0.5 * values * (1.0 + jax.scipy.special.erf(values * inv_root_two))


def gelu_slope(values):
    return (
        0.5 * (1.0 + jax.scipy.special.erf(values * inv_root_two))
        + values * jnp.exp(-0.5 * values * values) * inv_root_two_pi
    )


def span_mask(positions, starts):
    later = positions[:, None, :] <= positions[:, :, None]
    begin = starts[:, None]
    inside = (positions >= begin) & (positions < begin + PIC)
    return later | inside[:, :, None] & inside[:, None, :]


def project_rows(piece, weight):
    return jnp.einsum("ncd,de->nce", piece, weight, preferred_element_type=jnp.float32).astype(
        jnp.bfloat16
    )


def score_block(queries, key_rows, allowed):
    scores = jnp.einsum(
        "gqhe,gkhe->ghqk", queries, key_rows, preferred_element_type=jnp.float32
    ) * (1.0 / math.sqrt(HD))
    return jnp.where(allowed[:, None], scores, -1e30)


def shards(
    activations,
    routes,
    pic_start,
    router_w,
    gain_attn,
    gain_mlp,
    w_query,
    w_key,
    w_value,
    w_proj,
    w_up,
    w_down,
    cotangent,
):
    local_seqs = activations.shape[0]
    tensor_rank = lax.axis_index("tensor")
    own_routes = lax.dynamic_slice_in_dim(routes, tensor_rank * local_seqs, local_seqs, 0)
    gathered = (
        lax.all_gather(w_query, "dp", axis=0, tiled=True),
        lax.all_gather(w_key, "dp", axis=0, tiled=True),
        lax.all_gather(w_value, "dp", axis=0, tiled=True),
        lax.all_gather(w_proj, "dp", axis=0, tiled=True),
        lax.all_gather(w_up, "dp", axis=0, tiled=True),
        lax.all_gather(w_down, "dp", axis=0, tiled=True),
        lax.all_gather(router_w, "dp", axis=0, tiled=True),
        lax.all_gather(gain_attn, "dp", axis=0, tiled=True),
        lax.all_gather(gain_mlp, "dp", axis=0, tiled=True),
    )
    (
        full_query,
        full_key,
        full_value,
        full_proj,
        full_up,
        full_down,
        full_router,
        full_gain1,
        full_gain2,
    ) = gathered
    picks = own_routes[:, :, None]
    picked = jnp.take_along_axis(activations, picks, axis=1)
    picked_f32 = picked.astype(jnp.float32)
    gating = jax.nn.sigmoid(
        jnp.einsum("scd,d->sc", picked, full_router, preferred_element_type=jnp.float32)
    )
    normed1, inverse1 = normalize(picked_f32, full_gain1.astype(jnp.float32))
    piece = lax.all_gather(normed1.astype(jnp.bfloat16), "tensor", axis=0, tiled=True)
    norm_all = piece
    query_all = project_rows(piece, full_query)
    key_all = project_rows(piece, full_key)
    value_all = project_rows(piece, full_value)
    groups = query_all.shape[0]
    cap_rows = query_all.shape[1]
    heads = query_all.shape[2] // HD
    queries = query_all.reshape(groups, cap_rows, heads, HD)
    key_rows = key_all.reshape(groups, cap_rows, heads, HD)
    value_rows = value_all.reshape(groups, cap_rows, heads, HD)
    allowed = span_mask(routes, pic_start)
    scores = score_block(queries, key_rows, allowed)
    highest = jnp.max(scores, axis=-1, keepdims=True)
    log_total = highest + jnp.log(jnp.sum(jnp.exp(scores - highest), axis=-1, keepdims=True))
    attn_probs = jnp.exp(scores - log_total)
    context = jnp.einsum(
        "ghqk,gkhe->gqhe",
        attn_probs.astype(jnp.bfloat16),
        value_rows,
        preferred_element_type=jnp.float32,
    )
    context = context.astype(jnp.bfloat16).reshape(groups, cap_rows, heads * HD)
    part_rows = context
    attended = lax.psum_scatter(
        jnp.einsum("nce,de->ncd", part_rows, full_proj, preferred_element_type=jnp.float32),
        "tensor",
        scatter_dimension=0,
        tiled=True,
    )
    residual = picked_f32 + attended
    normed2, inverse2 = normalize(residual, full_gain2.astype(jnp.float32))
    piece = lax.all_gather(normed2.astype(jnp.bfloat16), "tensor", axis=0, tiled=True)
    pre_act = jnp.einsum("ncd,df->ncf", piece, full_up, preferred_element_type=jnp.float32)
    hidden = gelu_exact(pre_act).astype(jnp.bfloat16)
    part_rows = hidden
    mlp_out = lax.psum_scatter(
        jnp.einsum("ncf,df->ncd", part_rows, full_down, preferred_element_type=jnp.float32).astype(
            jnp.bfloat16
        ),
        "tensor",
        scatter_dimension=0,
        tiled=True,
    ).astype(jnp.float32)
    delta = attended + mlp_out
    new_rows = (picked_f32 + gating[..., None] * delta).astype(jnp.bfloat16)
    seq_lines = jnp.arange(local_seqs)[:, None]
    result = activations.at[seq_lines, own_routes].set(new_rows)
    pre_act = jnp.einsum("gcd,df->gcf", piece, full_up, preferred_element_type=jnp.float32)
    hidden = gelu_exact(pre_act).astype(jnp.bfloat16)
    grad_rows = jnp.take_along_axis(cotangent, picks, axis=1).astype(jnp.float32)
    grad_delta = gating[..., None] * grad_rows
    grad_gate = jnp.sum(grad_rows * delta, axis=-1)
    grad_score = grad_gate * gating * (1.0 - gating)
    branch_all = lax.all_gather(grad_delta.astype(jnp.bfloat16), "tensor", axis=0, tiled=True)
    grad_down = jnp.einsum("gcd,gcf->df", branch_all, hidden, preferred_element_type=jnp.float32)
    grad_hidden = jnp.einsum(
        "gcd,df->gcf", branch_all, full_down, preferred_element_type=jnp.float32
    )
    grad_pre = (grad_hidden * gelu_slope(pre_act)).astype(jnp.bfloat16)
    grad_up = jnp.einsum("gcd,gcf->df", piece, grad_pre, preferred_element_type=jnp.float32)
    part_rows = grad_pre
    grad_norm_two = lax.psum_scatter(
        jnp.einsum("ncf,df->ncd", part_rows, full_up, preferred_element_type=jnp.float32),
        "tensor",
        scatter_dimension=0,
        tiled=True,
    )
    grad_mid, grad_gain2 = norm_back(
        grad_norm_two, residual, inverse2, full_gain2.astype(jnp.float32)
    )
    grad_attended = (grad_delta + grad_mid).astype(jnp.bfloat16)
    attended_all = lax.all_gather(grad_attended, "tensor", axis=0, tiled=True)
    grad_proj = jnp.einsum("gcd,gce->de", attended_all, context, preferred_element_type=jnp.float32)
    grad_context = jnp.einsum(
        "gcd,de->gce", attended_all, full_proj, preferred_element_type=jnp.float32
    )
    grad_context = grad_context.astype(jnp.bfloat16).reshape(groups, cap_rows, heads, HD)
    attn_probs = jnp.exp(score_block(queries, key_rows, allowed) - log_total)
    grad_probs = jnp.einsum(
        "gqhe,gkhe->ghqk", grad_context, value_rows, preferred_element_type=jnp.float32
    )
    grad_scores = (
        attn_probs * (grad_probs - jnp.sum(attn_probs * grad_probs, axis=-1, keepdims=True))
    ).astype(jnp.bfloat16)
    grad_values = jnp.einsum(
        "ghqk,gqhe->gkhe",
        attn_probs.astype(jnp.bfloat16),
        grad_context,
        preferred_element_type=jnp.float32,
    )
    grad_values = grad_values.astype(jnp.bfloat16).reshape(groups, cap_rows, heads * HD)
    grad_queries = jnp.einsum(
        "ghqk,gkhe->gqhe", grad_scores, key_rows, preferred_element_type=jnp.float32
    ) * (1.0 / math.sqrt(HD))
    grad_queries = grad_queries.astype(jnp.bfloat16).reshape(groups, cap_rows, heads * HD)
    grad_keys = jnp.einsum(
        "ghqk,gqhe->gkhe", grad_scores, queries, preferred_element_type=jnp.float32
    ) * (1.0 / math.sqrt(HD))
    grad_keys = grad_keys.astype(jnp.bfloat16).reshape(groups, cap_rows, heads * HD)
    grad_query = jnp.einsum(
        "gcd,gce->de", norm_all, grad_queries, preferred_element_type=jnp.float32
    )
    grad_key = jnp.einsum("gcd,gce->de", norm_all, grad_keys, preferred_element_type=jnp.float32)
    grad_value = jnp.einsum(
        "gcd,gce->de", norm_all, grad_values, preferred_element_type=jnp.float32
    )
    total = jnp.einsum("nce,de->ncd", grad_queries, full_query, preferred_element_type=jnp.float32)
    total = total + jnp.einsum(
        "nce,de->ncd", grad_keys, full_key, preferred_element_type=jnp.float32
    )
    grad_norm_one = lax.psum_scatter(
        (
            total
            + jnp.einsum("nce,de->ncd", grad_values, full_value, preferred_element_type=jnp.float32)
        ).astype(jnp.bfloat16),
        "tensor",
        scatter_dimension=0,
        tiled=True,
    ).astype(jnp.float32)
    grad_picked_norm, grad_gain1 = norm_back(
        grad_norm_one, picked_f32, inverse1, full_gain1.astype(jnp.float32)
    )
    grad_router = jnp.einsum("sc,scd->d", grad_score, picked_f32)
    grad_picked = (
        grad_rows
        + grad_mid
        + grad_picked_norm
        + grad_score[..., None] * full_router.astype(jnp.float32)
    )
    grad_input = cotangent.at[seq_lines, own_routes].set(grad_picked.astype(jnp.bfloat16))
    summed = (
        lax.psum_scatter(grad_query, "dp", scatter_dimension=0, tiled=True),
        lax.psum_scatter(grad_key, "dp", scatter_dimension=0, tiled=True),
        lax.psum_scatter(grad_value, "dp", scatter_dimension=0, tiled=True),
        lax.psum_scatter(grad_proj, "dp", scatter_dimension=0, tiled=True),
        lax.psum_scatter(grad_up, "dp", scatter_dimension=0, tiled=True),
        lax.psum_scatter(grad_down, "dp", scatter_dimension=0, tiled=True),
        lax.psum_scatter(grad_router, "dp", scatter_dimension=0, tiled=True),
        lax.psum_scatter(grad_gain1, "dp", scatter_dimension=0, tiled=True),
        lax.psum_scatter(grad_gain2, "dp", scatter_dimension=0, tiled=True),
    )
    small = lax.psum((summed[6], summed[7], summed[8]), "tensor")
    return (
        result,
        grad_input,
        small[0],
        small[1],
        small[2],
        summed[0],
        summed[1],
        summed[2],
        summed[3],
        summed[4],
        summed[5],
    )


def solution(mesh):
    return jax.shard_map(
        shards,
        mesh=mesh,
        in_specs=(
            P(("dp", "tensor"), None, None),
            P("dp", None),
            P("dp"),
            P("dp"),
            P("dp"),
            P("dp"),
            P("dp", "tensor"),
            P("dp", "tensor"),
            P("dp", "tensor"),
            P("dp", "tensor"),
            P("dp", "tensor"),
            P("dp", "tensor"),
            P(("dp", "tensor"), None, None),
        ),
        out_specs=(
            P(("dp", "tensor"), None, None),
            P(("dp", "tensor"), None, None),
            P("dp"),
            P("dp"),
            P("dp"),
            P("dp", "tensor"),
            P("dp", "tensor"),
            P("dp", "tensor"),
            P("dp", "tensor"),
            P("dp", "tensor"),
            P("dp", "tensor"),
        ),
        check_vma=False,
    )
```

profile of v0, /device:TPU:0, one launch (start us, length us, event | category | flops | bytes accessed | tf_op | source)
XLA Modules:
  0.0 795.4 jit_solution(17995592886244408392)
XLA Ops:
  8.1 4.8 copy.118
  12.9 2.0 copy.119
  14.9 10.3 %all-gather.1 = bf16[8,1,128]{2,1,0:T(2,128)(2,1)S(1)} all-gather(bf16[1,1,128]{2,1,0:T(2,128)(2,1)S(1)} %bitcast.189), channel_id=1, replica_groups=mesh['dp'=8,'tensor'=4] {'dp'}, dimensions={0}, use_global_device_ids=true | all-gather | bytes 2304 | tf_op jit(solution)/shard_map/all_gather | solution.py:87
  25.2 3.4 gather_fusion
  29.0 1.0 fusion.24
  30.1 9.8 %all_gather.43 = bf16[1024,256]{1,0:T(8,128)(2,1)S(1)} all-gather(bf16[128,256]{1,0:T(8,128)(2,1)S(1)} %copy-done.26), channel_id=1, replica_groups=mesh['dp'=8,'tensor'=4] {'dp'}, dimensions={0}, use_global_device_ids=true | all-gather | bytes 589824 | tf_op jit(solution)/shard_map/all_gather | solution.py:80
  39.9 8.9 %all_gather.44 = bf16[1024,256]{1,0:T(8,128)(2,1)S(1)} all-gather(bf16[128,256]{1,0:T(8,128)(2,1)S(1)} %copy-done.27), channel_id=1, replica_groups=mesh['dp'=8,'tensor'=4] {'dp'}, dimensions={0}, use_global_device_ids=true | all-gather | bytes 589824 | tf_op jit(solution)/shard_map/all_gather | solution.py:81
  48.8 9.8 %all_gather.42 = bf16[1024,256]{1,0:T(8,128)(2,1)S(1)} all-gather(bf16[128,256]{1,0:T(8,128)(2,1)S(1)} %copy-done.28), channel_id=1, replica_groups=mesh['dp'=8,'tensor'=4] {'dp'}, dimensions={0}, use_global_device_ids=true | all-gather | bytes 589824 | tf_op jit(solution)/shard_map/all_gather | solution.py:82
  58.6 9.9 %all_gather.45 = bf16[1024,256]{1,0:T(8,128)(2,1)} all-gather(bf16[128,256]{1,0:T(8,128)(2,1)S(1)} %copy-done.29), channel_id=1, replica_groups=mesh['dp'=8,'tensor'=4] {'dp'}, dimensions={0}, use_global_device_ids=true | all-gather | bytes 589824 | tf_op jit(solution)/shard_map/all_gather | solution.py:83
  69.0 7.2 all-gather.10.cloned.1.call-done
  76.1 2.3 convolution_convert_fusion.3
  78.4 1.0 copy.74
  79.4 2.3 convolution_convert_fusion.4
  81.8 1.0 copy.73
  82.8 2.3 convolution_convert_fusion.5
  85.1 1.0 copy.72
  86.1 1.8 fusion.62
  88.8 0.8 copy-done.19
  89.6 2.7 fusion.39
  93.0 8.9 %all-gather.2 = bf16[8,1,128]{2,1,0:T(2,128)(2,1)S(1)} all-gather(bf16[1,1,128]{2,1,0:T(2,128)(2,1)S(1)} %bitcast.190), channel_id=1, replica_groups=mesh['dp'=8,'tensor'=4] {'dp'}, dimensions={0}, use_global_device_ids=true | all-gather | bytes 2304 | tf_op jit(solution)/shard_map/all_gather | solution.py:88
  101.9 4.1 gather_fusion.1
  106.0 8.7 %all-gather = bf16[8,1,128]{2,1,0:T(2,128)(2,1)S(1)} all-gather(bf16[1,1,128]{2,1,0:T(2,128)(2,1)S(1)} %bitcast.191), channel_id=1, replica_groups=mesh['dp'=8,'tensor'=4] {'dp'}, dimensions={0}, use_global_device_ids=true | all-gather | bytes 2304 | tf_op jit(solution)/shard_map/all_gather | solution.py:86
  115.1 53.0 %reduce-scatter.11.cloned.1.call-done = f32[2,128,1024]{2,1,0:T(8,128)} async-done(((f32[8,128,1024]{2,1,0:T(8,128)}), f32[2,128,1024]{2,1,0:T(8,128)}) %reduce-scatter.11.cloned.1.call-update) | async-done | bytes 1048592 | tf_op jit(solution)/shard_map/reduce_scatter | solution.py:132
  168.1 2.6 fusion.21
  170.8 1.0 multiply_convert_fusion.2
  173.2 44.7 %all-gather.12.cloned.1.call-done = bf16[8,128,1024]{2,1,0:T(8,128)(2,1)} async-done(((bf16[2,128,1024]{2,1,0:T(8,128)(2,1)}), bf16[8,128,1024]{2,1,0:T(8,128)(2,1)}) %all-gather.12.cloned.1.call-update) | async-done | bytes 2097168 | tf_op jit(solution)/shard_map/all_gather | solution.py:140
  218.0 7.4 multiply_convert_fusion
  225.4 20.9 %all-gather.16.cloned.1.call-done = bf16[1024,1024]{1,0:T(8,128)(2,1)} async-done(((bf16[128,1024]{1,0:T(8,128)(2,1)}), bf16[1024,1024]{1,0:T(8,128)(2,1)}) %all-gather.16.cloned.1.call-update) | async-done | bytes 2097168 | tf_op jit(solution)/shard_map/all_gather | solution.py:85
  246.2 47.1 %all-gather.18.cloned.1.call-done = bf16[8,128,1024]{2,1,0:T(8,128)(2,1)} async-done(((bf16[2,128,1024]{2,1,0:T(8,128)(2,1)}), bf16[8,128,1024]{2,1,0:T(8,128)(2,1)}) %all-gather.18.cloned.1.call-update) | async-done | bytes 2097168 | tf_op jit(solution)/shard_map/all_gather | solution.py:162
  293.4 6.3 fusion.5
  299.6 1.3 copy-done.39
  300.9 4.3 fusion.9
  305.3 75.7 %reduce-scatter.15.cloned.1.call-done = f32[2,128,1024]{2,1,0:T(8,128)} async-done(((f32[8,128,1024]{2,1,0:T(8,128)}), f32[2,128,1024]{2,1,0:T(8,128)}) %reduce-scatter.15.cloned.1.call-update) | async-done | bytes 1048592 | tf_op jit(solution)/shard_map/reduce_scatter | solution.py:170
  381.0 1.6 multiply_reduce_fusion.1
  382.7 1.3 fusion.31
  384.1 5.9 fusion.13
  390.4 39.9 %all-gather.20.cloned.1.call-done = bf16[8,128,1024]{2,1,0:T(8,128)(2,1)} async-done(((bf16[2,128,1024]{2,1,0:T(8,128)(2,1)}), bf16[8,128,1024]{2,1,0:T(8,128)(2,1)}) %all-gather.20.cloned.1.call-update) | async-done | bytes 2097168 | tf_op jit(solution)/shard_map/all_gather | solution.py:180
  430.2 3.2 convolution_convert_fusion.1
  433.4 2.0 copy.77
  435.4 1.9 multiply_reduce_fusion
  438.4 0.8 fusion.18
  439.9 0.8 convolution_convert_fusion
  442.1 0.8 fusion.41
  443.2 2.1 add_convert_fusion
  445.3 1.5 copy-done.36
  446.8 6.0 convolution_bitcast_fusion
  452.9 1.5 copy-done.35
  454.4 6.0 convolution_bitcast_fusion.1
  460.6 1.0 copy-done.20
  461.5 3.4 convolution_bitcast_fusion.2
  465.0 3.4 convolution_bitcast_fusion.3
  468.8 3.4 convolution_bitcast_fusion.5
  473.6 3.6 convolution_bitcast_fusion.4
  477.3 42.7 %reduce-scatter.17.cloned.1.call-done = bf16[2,128,1024]{2,1,0:T(8,128)(2,1)} async-done(((bf16[8,128,1024]{2,1,0:T(8,128)(2,1)}), bf16[2,128,1024]{2,1,0:T(8,128)(2,1)}) %reduce-scatter.17.cloned.1.call-update) | async-done | bytes 524304 | tf_op jit(solution)/shard_map/reduce_scatter | solution.py:219
  520.0 3.0 fusion.37
  522.9 37.1 %scatter_fusion = bf16[2,1024,1024]{2,1,0:T(8,128)(2,1)} fusion(bf16[2,1024,1024]{2,1,0:T(8,128)(2,1)} %copy.118, s32[256]{0:T(256)S(1)} %get-tuple-element.25, bf16[256,1024]{1,0:T(8,128)(2,1)} %bitcast.163), kind=kCustom, calls=%fused_computation.2 | custom fusion | bytes 1574912 | tf_op jit(solution)/shard_map/scatter | solution.py:155
  560.1 2.8 fusion.30
  562.9 36.9 %scatter_fusion.1 = bf16[2,1024,1024]{2,1,0:T(8,128)(2,1)} fusion(bf16[2,1024,1024]{2,1,0:T(8,128)(2,1)} %copy.119, s32[256]{0:T(256)S(1)} %get-tuple-element.25, bf16[256,1024]{1,0:T(8,128)(2,1)} %bitcast.162), kind=kCustom, calls=%fused_computation.3 | custom fusion | bytes 1574912 | tf_op jit(solution)/shard_map/scatter | solution.py:238
  600.0 24.8 %all-reduce.3 = (f32[1024]{0:T(1024)S(1)}, f32[1024]{0:T(1024)S(1)}, f32[1024]{0:T(1024)S(1)}) all-reduce(f32[1024]{0:T(1024)S(1)} %bitcast.186, f32[1024]{0:T(1024)S(1)} %get-tuple-element.14, f32[1024]{0:T(1024)S(1)} %get-tuple-element.12), channel_id=6, replica_groups=mesh['dp'=8,'tensor'=4] {'dp'}, use_global_device_ids=true, to_apply=%region_14.16.clone | all-reduce | flops 3072 | bytes 24576
  625.0 10.4 %all-reduce.4 = (f32[128]{0:T(128)}, f32[128]{0:T(128)}, f32[128]{0:T(128)}) all-reduce(f32[128]{0:T(128)S(1)} %dynamic-slice.1, f32[128]{0:T(128)S(1)} %dynamic-slice.3, f32[128]{0:T(128)S(1)} %dynamic-slice.5), channel_id=1, replica_groups=mesh['dp'=8,'tensor'=4] {'tensor'}, use_global_device_ids=true, to_apply=%region_15.17 | all-reduce | flops 384 | bytes 3072 | tf_op jit(solution)/shard_map/psum | solution.py:250
  635.4 33.4 %reduce-scatter.25.cloned.1.call-done = f32[128,256]{1,0:T(8,128)} async-done(((f32[1024,256]{1,0:T(8,128)}), f32[128,256]{1,0:T(8,128)}) %reduce-scatter.25.cloned.1.call-update) | async-done | bytes 131088 | tf_op jit(solution)/shard_map/reduce_scatter | solution.py:243
  668.9 39.6 %reduce-scatter.23.cloned.1.call-done = f32[128,256]{1,0:T(8,128)} async-done(((f32[1024,256]{1,0:T(8,128)}), f32[128,256]{1,0:T(8,128)}) %reduce-scatter.23.cloned.1.call-update) | async-done | bytes 131088 | tf_op jit(solution)/shard_map/reduce_scatter | solution.py:242
  708.5 39.7 %reduce-scatter.19.cloned.1.call-done = f32[128,256]{1,0:T(8,128)} async-done(((f32[1024,256]{1,0:T(8,128)}), f32[128,256]{1,0:T(8,128)}) %reduce-scatter.19.cloned.1.call-update) | async-done | bytes 131088 | tf_op jit(solution)/shard_map/reduce_scatter | solution.py:240
  748.1 39.5 %reduce-scatter.21.cloned.1.call-done = f32[128,256]{1,0:T(8,128)} async-done(((f32[1024,256]{1,0:T(8,128)}), f32[128,256]{1,0:T(8,128)}) %reduce-scatter.21.cloned.1.call-update) | async-done | bytes 131088 | tf_op jit(solution)/shard_map/reduce_scatter | solution.py:241
  (140 shorter events, 9.8 us)
Async XLA Ops:
  8.0 68.1 %all-gather.10.cloned.1.call-start = ((), (), s32[]{:S(2)}) async-start(), calls=%async_computation.10 | async-start | bytes 2621440 | tf_op jit(solution)/shard_map/all_gather | solution.py:108
  8.1 4.8 copy-start.11
  12.9 2.0 copy-start.30
  12.9 2.1 copy-start.31
  28.6 86.2 %copy-start = (bf16[256,1024]{1,0:T(8,128)(2,1)}, bf16[256,1024]{1,0:T(8,128)(2,1)S(1)}, u32[]{:S(2)}) copy-start(bf16[256,1024]{1,0:T(8,128)(2,1)S(1)} %gather_fusion) | copy-start | bytes 1572868
  28.6 1.5 copy-start.26
  28.6 11.3 %copy-start.27 = (bf16[128,256]{1,0:T(8,128)(2,1)S(1)}, bf16[128,256]{1,0:T(8,128)(2,1)}, u32[]{:S(2)}) copy-start(bf16[128,256]{1,0:T(8,128)(2,1)} %param.22) | copy-start | bytes 196612
  28.6 20.2 %copy-start.28 = (bf16[128,256]{1,0:T(8,128)(2,1)S(1)}, bf16[128,256]{1,0:T(8,128)(2,1)}, u32[]{:S(2)}) copy-start(bf16[128,256]{1,0:T(8,128)(2,1)} %param.23) | copy-start | bytes 196612
  28.6 30.0 %copy-start.29 = (bf16[128,256]{1,0:T(8,128)(2,1)S(1)}, bf16[128,256]{1,0:T(8,128)(2,1)}, u32[]{:S(2)}) copy-start(bf16[128,256]{1,0:T(8,128)(2,1)} %param.24) | copy-start | bytes 196612
  28.9 39.6 %copy-start.32 = (s32[8]{0:T(128)S(1)}, s32[8]{0:T(128)}, u32[]{:S(2)}) copy-start(s32[8]{0:T(128)} %param.17) | copy-start | bytes 100
  30.0 138.0 %reduce-scatter.11.cloned.1.call-start = ((), (), s32[]{:S(2)}) async-start(), calls=%async_computation.11 | async-start | bytes 5242880 | tf_op jit(solution)/shard_map/reduce_scatter | solution.py:132
  39.9 39.5 %copy-start.16 = (bf16[1024,256]{1,0:T(8,128)(2,1)}, bf16[1024,256]{1,0:T(8,128)(2,1)S(1)}, u32[]{:S(2)}) copy-start(bf16[1024,256]{1,0:T(8,128)(2,1)S(1)} %all_gather.43) | copy-start | bytes 1572868
  48.8 29.7 %copy-start.14 = (bf16[1024,256]{1,0:T(8,128)(2,1)}, bf16[1024,256]{1,0:T(8,128)(2,1)S(1)}, u32[]{:S(2)}) copy-start(bf16[1024,256]{1,0:T(8,128)(2,1)S(1)} %all_gather.44) | copy-start | bytes 1572868
  58.6 24.2 %copy-start.12 = (bf16[1024,256]{1,0:T(8,128)(2,1)}, bf16[1024,256]{1,0:T(8,128)(2,1)S(1)}, u32[]{:S(2)}) copy-start(bf16[1024,256]{1,0:T(8,128)(2,1)S(1)} %all_gather.42) | copy-start | bytes 1572868
  86.1 2.3 copy-start.8
  88.3 1.3 copy-start.18
  88.8 0.8 copy-start.19
  92.3 0.7 copy-start.33
  92.3 80.9 %all-gather.14.cloned.1.call-start = ((), (), s32[]{:S(2)}) async-start(), calls=%async_computation.13 | async-start | bytes 2359296 | tf_op jit(solution)/shard_map/all_gather | solution.py:84
  92.9 125.1 %all-gather.12.cloned.1.call-start = ((), (), s32[]{:S(2)}) async-start(), calls=%async_computation.12 | async-start | bytes 2621440 | tf_op jit(solution)/shard_map/all_gather | solution.py:140
  101.9 4.1 copy-start.34
  171.8 74.4 %all-gather.16.cloned.1.call-start = ((), (), s32[]{:S(2)}) async-start(), calls=%async_computation.14 | async-start | bytes 2359296 | tf_op jit(solution)/shard_map/all_gather | solution.py:85
  172.4 121.0 %all-gather.18.cloned.1.call-start = ((), (), s32[]{:S(2)}) async-start(), calls=%async_computation.16 | async-start | bytes 2621440 | tf_op jit(solution)/shard_map/all_gather | solution.py:162
  173.1 207.9 %reduce-scatter.15.cloned.1.call-start = ((), (), s32[]{:S(2)}) async-start(), calls=%async_computation.17 | async-start | bytes 5242880 | tf_op jit(solution)/shard_map/reduce_scatter | solution.py:170
  293.4 7.6 copy-start.37
  299.6 1.3 copy-start.39
  305.3 124.9 %all-gather.20.cloned.1.call-start = ((), (), s32[]{:S(2)}) async-start(), calls=%async_computation.18 | async-start | bytes 2621440 | tf_op jit(solution)/shard_map/all_gather | solution.py:180
  381.0 1.7 copy-start.2
  381.0 1.7 copy-start.4
  384.1 93.2 %reduce-scatter.13.cloned.1.call-start = ((), (), s32[]{:S(2)}) async-start(), calls=%async_computation.15 | async-start | bytes 2621440 | tf_op jit(solution)/shard_map/reduce_scatter | solution.py:144
  390.1 129.9 %reduce-scatter.17.cloned.1.call-start = ((), (), s32[]{:S(2)}) async-start(), calls=%async_computation.19 | async-start | bytes 2621440 | tf_op jit(solution)/shard_map/reduce_scatter | solution.py:219
  437.3 1.1 copy-start.7
  438.4 1.0 copy-start.6
  438.4 1.5 copy-start.9
  439.4 2.4 copy-start.21
  439.9 2.0 copy-start.22
  439.9 1.2 copy-start.17
  440.7 2.2 copy-start.24
  441.1 1.0 copy-start.15
  442.1 1.0 copy-start.13
  445.3 1.6 copy-start.36
  445.3 190.2 %reduce-scatter.29.cloned.1.call-start = ((), (), s32[]{:S(2)}) async-start(), calls=%async_computation.25 | async-start | bytes 4718592 | tf_op jit(solution)/shard_map/reduce_scatter | solution.py:245
  452.8 1.6 copy-start.35
  452.9 182.6 %reduce-scatter.27.cloned.1.call-start = ((), (), s32[]{:S(2)}) async-start(), calls=%async_computation.24 | async-start | bytes 4718592 | tf_op jit(solution)/shard_map/reduce_scatter | solution.py:244
  460.5 1.1 copy-start.20
  460.5 4.5 copy-start.25
  460.5 208.4 %reduce-scatter.25.cloned.1.call-start = ((), (), s32[]{:S(2)}) async-start(), calls=%async_computation.23 | async-start | bytes 1179648 | tf_op jit(solution)/shard_map/reduce_scatter | solution.py:243
  465.0 3.8 copy-start.23
  465.0 243.5 %reduce-scatter.23.cloned.1.call-start = ((), (), s32[]{:S(2)}) async-start(), calls=%async_computation.22 | async-start | bytes 1179648 | tf_op jit(solution)/shard_map/reduce_scatter | solution.py:242
  468.5 3.9 copy-start.38
  468.5 279.6 %reduce-scatter.19.cloned.1.call-start = ((), (), s32[]{:S(2)}) async-start(), calls=%async_computation.20 | async-start | bytes 1179648 | tf_op jit(solution)/shard_map/reduce_scatter | solution.py:240
  472.2 315.4 %reduce-scatter.21.cloned.1.call-start = ((), (), s32[]{:S(2)}) async-start(), calls=%async_computation.21 | async-start | bytes 1179648 | tf_op jit(solution)/shard_map/reduce_scatter | solution.py:241
  473.6 46.4 %copy-start.1 = (bf16[256,1024]{1,0:T(8,128)(2,1)S(1)}, bf16[256,1024]{1,0:T(8,128)(2,1)}, u32[]{:S(2)}) copy-start(bf16[256,1024]{1,0:T(8,128)(2,1)} %copy-done) | copy-start | bytes 1572868
  473.6 46.4 %copy-start.3 = (bf16[256,1024]{1,0:T(8,128)(2,1)S(1)}, bf16[256,1024]{1,0:T(8,128)(2,1)}, u32[]{:S(2)}) copy-start(bf16[256,1024]{1,0:T(8,128)(2,1)} %gather_fusion.1) | copy-start | bytes 1572868
  473.6 46.4 %copy-start.10 = (f32[2,128,1024]{2,1,0:T(8,128)S(1)}, f32[2,128,1024]{2,1,0:T(8,128)}, u32[]{:S(2)}) copy-start(f32[2,128,1024]{2,1,0:T(8,128)} %reduce-scatter.11.cloned.1.call-done) | copy-start | bytes 3145732
  522.9 37.2 %copy-start.5 = (f32[2,128,1024]{2,1,0:T(8,128)S(1)}, f32[2,128,1024]{2,1,0:T(8,128)}, u32[]{:S(2)}) copy-start(f32[2,128,1024]{2,1,0:T(8,128)} %reduce-scatter.15.cloned.1.call-done) | copy-start | bytes 3145732
Sparse Core Ops, SparseCore 0:
  30.1 45.9 all-gather.9
  92.4 75.5 reduce-scatter.10
  305.4 75.5 reduce-scatter.14
Sparse Core Ops, SparseCore 1:
  94.7 26.4 all-gather.13
  171.9 46.0 all-gather.11
  219.7 26.4 all-gather.15
  247.8 45.5 all-gather.17
  384.2 46.0 all-gather.19
  432.5 42.4 reduce-scatter.12
  477.1 42.8 reduce-scatter.16
  523.8 50.1 reduce-scatter.28
  577.7 51.4 reduce-scatter.26
  633.0 35.9 reduce-scatter.24
  672.5 35.9 reduce-scatter.22
  712.2 35.9 reduce-scatter.18
  751.8 35.9 reduce-scatter.20
where the time goes:
time: 807 us; the launch traced here: 795 us
  waiting for transfers between devices  485 us (60%)
  local copies, waits for them, and re-layouts  102 us (13%)
  blocking collectives  102 us (13%)
  matrix products  72.9 us (9%)
  between operations  17.1 us (2%)
  other arithmetic  15.3 us (2%)
    reduce_scatter x1, waiting for transfers between devices, shards(): lax.psum_scatter(jnp.einsum('ncf,df->ncd', part_rows, full_up, preferred_...  75.7 us
    reduce_scatter x1, waiting for transfers between devices, shards(): lax.psum_scatter(jnp.einsum('nce,de->ncd', part_rows, full_proj, preferre...  53 us
    all_gather x1, waiting for transfers between devices, shards(): lax.all_gather(grad_delta.astype(jnp.bfloat16), 'tensor', axis=0, tiled=T...  47.1 us
    all_gather x1, waiting for transfers between devices, shards(): lax.all_gather(normed2.astype(jnp.bfloat16), 'tensor', axis=0, tiled=True)  44.7 us
    reduce_scatter x1, waiting for transfers between devices, shards(): lax.psum_scatter((total + jnp.einsum('nce,de->ncd', grad_values, full_val...  42.7 us
    all_gather x1, waiting for transfers between devices, shards(): attended_all = lax.all_gather(grad_attended, 'tensor', axis=0, tiled=True)  39.9 us
    reduce_scatter x1, waiting for transfers between devices, shards(): lax.psum_scatter(grad_query, 'dp', scatter_dimension=0, tiled=True)  39.7 us
    reduce_scatter x1, waiting for transfers between devices, shards(): lax.psum_scatter(grad_value, 'dp', scatter_dimension=0, tiled=True)  39.6 us
  transfers between devices with their start and end apart: 16, of which 12 were waited for; matrix products, arithmetic and copies ran while one was open for 18% of the time, Pallas kernels for 0%

commit v1 on v0

v1 whole, which is shorter than its diff:
```python
import functools
import math

import jax
import jax.numpy as jnp
from jax import lax
from jax.experimental import pallas as pl
from jax.experimental.pallas import tpu as pltpu
from jax.sharding import PartitionSpec as P

HD = 64
PIC = 256
AHEAD = 1
MESH = pl.DeviceIdType.MESH
ANY = pl.BlockSpec(memory_space=pl.ANY)
VMEM = pl.BlockSpec(memory_space=pltpu.VMEM)
BF16 = jnp.bfloat16
F32 = jnp.float32

inv_root_two = 0.7071067811865476
inv_root_two_pi = 0.3989422804014327


def bit_of(value, bit):
    return lax.rem(lax.div(value, 1 << bit), 2)


def flipped(value, bit):
    return value + (1 - 2 * bit_of(value, bit)) * (1 << bit)


def cleared(value, bits):
    for bit in bits:
        value = value - bit_of(value, bit) * (1 << bit)
    return value


def spread(step, bits):
    value = 0
    for place, bit in enumerate(bits):
        value = value + lax.rem(lax.div(step, 1 << place), 2) * (1 << bit)
    return value


def each(count, body):
    if count <= 4:
        for step in range(count):
            body(jnp.int32(step))
    else:
        lax.fori_loop(0, count, lambda step, _: body(step), None)


def orders(bits):
    return (tuple(range(bits - 1, 0, -1)), tuple(range(1, bits)))


def meet(bits, ranks):
    me, rank = lax.axis_index("dp"), lax.axis_index("tensor")
    barrier = pltpu.get_barrier_semaphore()
    for bit in range(bits):
        pl.semaphore_signal(barrier, 1, device_id=(flipped(me, bit), rank), device_id_type=MESH)
    for hop in range(1, ranks):
        pl.semaphore_signal(
            barrier, 1, device_id=(me, lax.rem(rank + hop, ranks)), device_id_type=MESH
        )
    pl.semaphore_wait(barrier, bits + ranks - 1)


def remote(src, dst, send, recv, where):
    return pltpu.make_async_remote_copy(
        src_ref=src, dst_ref=dst, send_sem=send, recv_sem=recv, device_id=where, device_id_type=MESH
    )


def gather_kernel(bits, ranks, chunks, *refs):
    shards, (vec,) = refs[:chunks], refs[chunks : chunks + 1]
    wholes = refs[chunks + 1 : 2 * chunks + 1]
    (
        vec_out,
        held,
        vecs,
        send_z,
        recv_z,
        send_p,
        recv_p,
        send_c,
        recv_c,
        send_v,
        recv_v,
        local,
        leave,
    ) = refs[2 * chunks + 1 :]
    me, rank = lax.axis_index("dp"), lax.axis_index("tensor")
    rows, width = shards[0].shape
    full = held.shape[2]
    half = full // 2
    paths = orders(bits)
    meet(bits, ranks)

    def band(index):
        return pl.ds(pl.multiple_of(index * rows, rows), rows)

    mine = band(me)
    columns = pl.ds(pl.multiple_of(rank * width, width), width)
    for chunk in range(chunks):
        pltpu.make_async_copy(shards[chunk], held.at[chunk, mine, columns], local.at[chunk]).start()
    pltpu.make_async_copy(vec, vecs.at[me], local.at[chunks]).start()
    for chunk in range(chunks):
        for hop in range(1, ranks):
            remote(
                shards[chunk],
                held.at[chunk, mine, columns],
                send_z.at[chunk],
                recv_z.at[chunk],
                (me, lax.rem(rank + hop, ranks)),
            ).start()
    pltpu.make_async_copy(vec, vecs.at[me], local.at[chunks]).wait()
    path = tuple(range(bits - 1, -1, -1))
    for stage, bit in enumerate(path):
        other = (flipped(me, bit), rank)

        def send(step, stage=stage, other=other):
            index = cleared(me, path[:stage]) + spread(step, path[:stage])
            remote(
                vecs.at[index], vecs.at[index], send_v.at[stage], recv_v.at[stage], other
            ).start()

        each(1 << stage, send)
        span = vecs.at[pl.ds(0, 1 << stage)]
        remote(span, span, send_v.at[stage], recv_v.at[stage], other).wait()

    def bulk(chunk, depth, breadth):
        return held.at[chunk, pl.ds(0, depth), pl.ds(0, breadth)]

    def wait_z(chunk):
        pltpu.make_async_copy(
            shards[chunk], held.at[chunk, mine, columns], local.at[chunk]
        ).wait()
        span = bulk(chunk, rows, width * (ranks - 1))
        remote(span, span, send_z.at[chunk], recv_z.at[chunk], (me, rank)).wait_recv()

    def send_path(chunk, colour, stage):
        order = paths[colour]
        other = (flipped(me, order[stage]), rank)

        def send(step):
            index = cleared(me, order[:stage]) + spread(step, order[:stage])
            block = held.at[chunk, band(index), pl.ds(colour * half, half)]
            remote(
                block,
                block,
                send_p.at[chunk, colour, stage],
                recv_p.at[chunk, colour, stage],
                other,
            ).start()

        each(1 << stage, send)

    def path_copy(chunk, colour, stage):
        span = bulk(chunk, rows << stage, half)
        return remote(
            span,
            span,
            send_p.at[chunk, colour, stage],
            recv_p.at[chunk, colour, stage],
            (me, rank),
        )

    def send_core(chunk):
        other = (flipped(me, 0), rank)

        def send(step):
            index = cleared(me, range(1, bits)) + spread(step, range(1, bits))
            block = held.at[chunk, band(index)]
            remote(block, block, send_c.at[chunk], recv_c.at[chunk], other).start()

        each(1 << (bits - 1), send)

    def core_copy(chunk):
        span = bulk(chunk, rows << (bits - 1), full)
        return remote(span, span, send_c.at[chunk], recv_c.at[chunk], (me, rank))

    last = bits
    for tick in range(chunks + AHEAD * last):
        for stage in range(last, -1, -1):
            chunk = tick - AHEAD * stage
            if not 0 <= chunk < chunks:
                continue
            if stage == 0:
                wait_z(chunk)
            elif stage < last:
                for colour in range(2):
                    path_copy(chunk, colour, stage - 1).wait_recv()
            else:
                core_copy(chunk).wait_recv()
            if stage < last - 1:
                for colour in range(2):
                    send_path(chunk, colour, stage)
            elif stage == last - 1:
                send_core(chunk)
            else:
                pltpu.make_async_copy(held.at[chunk], wholes[chunk], leave.at[chunk]).start()
    vec_out[...] = vecs[...]
    for chunk in range(chunks):
        pltpu.make_async_copy(held.at[chunk], wholes[chunk], leave.at[chunk]).wait()
        span = bulk(chunk, rows, width * (ranks - 1))
        remote(span, span, send_z.at[chunk], recv_z.at[chunk], (me, rank)).wait_send()
        for colour in range(2):
            for stage in range(bits - 1):
                path_copy(chunk, colour, stage).wait_send()
        core_copy(chunk).wait_send()


def gather_weights(bits, ranks, shards, vec):
    chunks = len(shards)
    rows, width = shards[0].shape
    depth, breadth = rows << bits, width * ranks
    dma = pltpu.SemaphoreType.DMA
    outs = pl.pallas_call(
        functools.partial(gather_kernel, bits, ranks, chunks),
        out_shape=[jax.ShapeDtypeStruct((depth, breadth), BF16)] * chunks
        + [jax.ShapeDtypeStruct((1 << bits, 8, 128), F32)],
        in_specs=[ANY] * chunks + [VMEM],
        out_specs=[ANY] * chunks + [VMEM],
        scratch_shapes=[
            pltpu.VMEM((chunks, depth, breadth), BF16),
            pltpu.VMEM((1 << bits, 8, 128), F32),
            dma((chunks,)),
            dma((chunks,)),
            dma((chunks, 2, bits - 1)),
            dma((chunks, 2, bits - 1)),
            dma((chunks,)),
            dma((chunks,)),
            dma((bits,)),
            dma((bits,)),
            dma((chunks + 1,)),
            dma((chunks,)),
        ],
        compiler_params=pltpu.CompilerParams(
            collective_id=1, has_side_effects=True, vmem_limit_bytes=60 << 20
        ),
        name="gather_weights",
    )(*shards, vec)
    return outs[:chunks], outs[chunks]


def scatter_kernel(bits, ranks, chunks, *refs):
    grads, (vec,) = refs[:chunks], refs[chunks : chunks + 1]
    outs = refs[chunks + 1 : 2 * chunks + 1]
    (
        vec_out,
        total,
        from_core,
        *from_path,
        from_z,
        vecs,
        vec_path,
        vec_z,
        send_c,
        recv_c,
        send_p,
        recv_p,
        send_z,
        recv_z,
        send_v,
        recv_v,
        local,
    ) = refs[2 * chunks + 1 :]
    me, rank = lax.axis_index("dp"), lax.axis_index("tensor")
    rows, width = outs[0].shape
    full = total.shape[3]
    half = full // 2
    seat, pair = bit_of(me, 0), lax.div(me, 2)
    pairs = 1 << (bits - 1)
    paths = tuple(tuple(bit - 1 for bit in order[::-1]) for order in orders(bits))
    meet(bits, ranks)

    def band(index):
        return pl.ds(pl.multiple_of(index * rows, rows), rows)

    for chunk in range(chunks):

        def send(step, chunk=chunk):
            remote(
                grads[chunk].at[band(2 * step + 1 - seat)],
                from_core.at[chunk, step],
                send_c.at[chunk],
                recv_c.at[chunk],
                (flipped(me, 0), rank),
            ).start()
            pltpu.make_async_copy(
                grads[chunk].at[band(2 * step + seat)], total.at[chunk, step], local.at[chunk]
            ).start()

        each(pairs, send)

    def core_copy(chunk):
        span = from_core.at[chunk]
        return remote(span, span, send_c.at[chunk], recv_c.at[chunk], (me, rank))

    tile = min(rows, 32)

    def add_to(chunk, index, columns, source):
        for start in range(0, rows, tile):
            part = pl.ds(start, tile)
            here = total.at[chunk, index, part, columns]
            here[...] = (here[...].astype(F32) + source[part].astype(F32)).astype(BF16)

    def add_core(chunk):
        lax.fori_loop(
            0,
            pairs,
            lambda step, _: add_to(chunk, step, pl.ds(0, full), from_core.at[chunk, step]),
            None,
        )

    def members(stage, order, step, kept):
        bit, later = order[stage], order[stage + 1 :]
        index = pair if kept else flipped(pair, bit)
        return cleared(index, later) + spread(step, later)

    def send_path(chunk, colour, stage):
        order = paths[colour]
        other = (2 * flipped(pair, order[stage]) + seat, rank)

        def send(step):
            index = members(stage, order, step, False)
            remote(
                total.at[chunk, index, :, pl.ds(colour * half, half)],
                from_path[stage].at[chunk, colour, step],
                send_p.at[chunk, colour, stage],
                recv_p.at[chunk, colour, stage],
                other,
            ).start()

        each(1 << (len(order) - stage - 1), send)

    def path_copy(chunk, colour, stage):
        span = from_path[stage].at[chunk, colour]
        return remote(
            span,
            span,
            send_p.at[chunk, colour, stage],
            recv_p.at[chunk, colour, stage],
            (me, rank),
        )

    def add_path(chunk, colour, stage):
        order = paths[colour]

        def add(step, _):
            index = members(stage, order, step, True)
            add_to(
                chunk,
                index,
                pl.ds(colour * half, half),
                from_path[stage].at[chunk, colour, step],
            )

        lax.fori_loop(0, 1 << (len(order) - stage - 1), add, None)

    def send_across(chunk):
        for hop in range(1, ranks):
            to = lax.rem(rank + hop, ranks)
            remote(
                total.at[chunk, pair, :, pl.ds(pl.multiple_of(to * width, width), width)],
                from_z.at[chunk, hop - 1],
                send_z.at[chunk],
                recv_z.at[chunk],
                (me, to),
            ).start()

    def z_copy(chunk):
        span = from_z.at[chunk]
        return remote(span, span, send_z.at[chunk], recv_z.at[chunk], (me, rank))

    def finish(chunk):
        own = total[chunk, pair, :, pl.ds(pl.multiple_of(rank * width, width), width)]
        summed = own.astype(F32)
        for hop in range(1, ranks):
            summed = summed + from_z[chunk, hop - 1].astype(F32)
        outs[chunk][...] = summed

    last = bits
    for tick in range(chunks + AHEAD * last):
        for stage in range(last, -1, -1):
            chunk = tick - AHEAD * stage
            if not 0 <= chunk < chunks:
                continue
            if stage == 0:
                span = total.at[chunk]
                pltpu.make_async_copy(span, span, local.at[chunk]).wait()
                core_copy(chunk).wait_recv()
                add_core(chunk)
            elif stage < last:
                for colour in range(2):
                    path_copy(chunk, colour, stage - 1).wait_recv()
                    add_path(chunk, colour, stage - 1)
            else:
                z_copy(chunk).wait_recv()
                finish(chunk)
            if stage < last - 1:
                for colour in range(2):
                    send_path(chunk, colour, stage)
            elif stage == last - 1:
                send_across(chunk)
    pltpu.make_async_copy(vec, vecs, local.at[chunks]).start()
    pltpu.make_async_copy(vec, vecs, local.at[chunks]).wait()
    path = tuple(range(bits))
    for stage, bit in enumerate(path):
        later = path[stage + 1 :]
        count = 1 << len(later)
        base = count - 1
        other = (flipped(me, bit), rank)

        def send(step, later=later, bit=bit, base=base, other=other, stage=stage):
            index = cleared(flipped(me, bit), later) + spread(step, later)
            remote(
                vecs.at[index], vec_path.at[base + step], send_v.at[stage], recv_v.at[stage], other
            ).start()

        each(count, send)
        span = vec_path.at[pl.ds(base, count)]
        remote(span, span, send_v.at[stage], recv_v.at[stage], other).wait()

        def add(step, _, later=later, base=base):
            index = cleared(me, later) + spread(step, later)
            vecs[index] = vecs[index] + vec_path[base + step]

        lax.fori_loop(0, count, add, None)
    for hop in range(1, ranks):
        to = (me, lax.rem(rank + hop, ranks))
        remote(vecs.at[me], vec_z.at[hop - 1], send_v.at[bits], recv_v.at[bits], to).start()
    remote(vec_z, vec_z, send_v.at[bits], recv_v.at[bits], (me, rank)).wait()
    summed = vecs[me]
    for hop in range(1, ranks):
        summed = summed + vec_z[hop - 1]
    vec_out[...] = summed
    for chunk in range(chunks):
        core_copy(chunk).wait_send()
        for colour in range(2):
            for stage in range(bits - 1):
                path_copy(chunk, colour, stage).wait_send()
        z_copy(chunk).wait_send()


def scatter_grads(bits, ranks, grads, vec):
    chunks = len(grads)
    depth, breadth = grads[0].shape
    rows, width, pairs = depth >> bits, breadth // ranks, 1 << (bits - 1)
    dma = pltpu.SemaphoreType.DMA
    outs = pl.pallas_call(
        functools.partial(scatter_kernel, bits, ranks, chunks),
        out_shape=[jax.ShapeDtypeStruct((rows, width), F32)] * chunks
        + [jax.ShapeDtypeStruct((8, 128), F32)],
        in_specs=[ANY] * chunks + [VMEM],
        out_specs=[VMEM] * (chunks + 1),
        scratch_shapes=[
            pltpu.VMEM((chunks, pairs, rows, breadth), BF16),
            pltpu.VMEM((chunks, pairs, rows, breadth), BF16),
            *[
                pltpu.VMEM((chunks, 2, pairs >> (stage + 1), rows, breadth // 2), BF16)
                for stage in range(bits - 1)
            ],
            pltpu.VMEM((chunks, ranks - 1, rows, width), BF16),
            pltpu.VMEM((1 << bits, 8, 128), F32),
            pltpu.VMEM((1 << bits, 8, 128), F32),
            pltpu.VMEM((ranks - 1, 8, 128), F32),
            dma((chunks,)),
            dma((chunks,)),
            dma((chunks, 2, bits - 1)),
            dma((chunks, 2, bits - 1)),
            dma((chunks,)),
            dma((chunks,)),
            dma((bits + 1,)),
            dma((bits + 1,)),
            dma((chunks + 1,)),
        ],
        compiler_params=pltpu.CompilerParams(
            collective_id=2, has_side_effects=True, vmem_limit_bytes=60 << 20
        ),
        name="scatter_grads",
    )(*grads, vec)
    return outs[:chunks], outs[chunks]


def normalize(values, gain):
    inverse = lax.rsqrt(jnp.mean(values * values, axis=-1, keepdims=True) + 1e-06)
    return (values * inverse * gain, inverse)


def norm_back(grad_out, values, inverse, gain):
    scaled = grad_out * gain
    grad_in = inverse * scaled - values * inverse * inverse * inverse * jnp.mean(
        scaled * values, axis=-1, keepdims=True
    )
    grad_gain = jnp.sum(grad_out * values * inverse, axis=0)
    return (grad_in, grad_gain)


def gelu_parts(values):
    bell = 0.5 * (1.0 + jax.scipy.special.erf(values * inv_root_two))
    slope = bell + values * jnp.exp(-0.5 * values * values) * inv_root_two_pi
    return (values * bell).astype(BF16), slope


def span_mask(positions, starts):
    later = positions[:, None, :] <= positions[:, :, None]
    begin = starts[:, None]
    inside = (positions >= begin) & (positions < begin + PIC)
    return later | inside[:, :, None] & inside[:, None, :]


def dot(form, left, right):
    return jnp.einsum(form, left, right, preferred_element_type=F32)


def shards(
    activations,
    routes,
    pic_start,
    router_w,
    gain_attn,
    gain_mlp,
    w_query,
    w_key,
    w_value,
    w_proj,
    w_up,
    w_down,
    cotangent,
):
    seqs, length, features = activations.shape
    ranks = lax.axis_size("tensor")
    bits = lax.axis_size("dp").bit_length() - 1
    rank = lax.axis_index("tensor")
    rows, width = w_query.shape
    parts = w_up.shape[1] // width
    own_routes = lax.dynamic_slice_in_dim(routes, rank * seqs, seqs, 0)
    own_start = lax.dynamic_slice_in_dim(pic_start, rank * seqs, seqs, 0)
    caps = routes.shape[1]
    heads = features // HD

    vec = jnp.stack([router_w, gain_attn, gain_mlp]).astype(F32)
    vec = jnp.pad(vec, ((0, 5), (0, 128 - rows)))
    pieces = [w_query, w_key, w_value, w_proj]
    for part in range(parts):
        columns = slice(part * width, (part + 1) * width)
        pieces += [w_up[:, columns], w_down[:, columns]]
    weights, vec_all = gather_weights(bits, ranks, pieces, vec)
    full_query, full_key, full_value, full_proj = weights[:4]
    full_up, full_down = weights[4::2], weights[5::2]
    vec_all = vec_all[:, :3, :rows].transpose(1, 0, 2).reshape(3, features)
    router, gain1, gain2 = vec_all[0], vec_all[1], vec_all[2]

    chosen = (own_routes[:, :, None] == jnp.arange(length)[None, None, :]).astype(BF16)
    picked = dot("scl,sld->scd", chosen, activations).reshape(seqs * caps, features)
    grad_rows = dot("scl,sld->scd", chosen, cotangent).reshape(seqs * caps, features)
    gating = jax.nn.sigmoid(jnp.sum(picked * router, axis=-1, keepdims=True))
    grad_delta = gating * grad_rows
    branch = grad_delta.astype(BF16)

    normed1, inverse1 = normalize(picked, gain1)
    norm_one = normed1.astype(BF16)
    queries = dot("nd,de->ne", norm_one, full_query).astype(BF16)
    key_rows = dot("nd,de->ne", norm_one, full_key).astype(BF16)
    value_rows = dot("nd,de->ne", norm_one, full_value).astype(BF16)
    split = lambda a: a.reshape(seqs, caps, heads, HD)
    allowed = span_mask(own_routes, own_start)
    scores = dot("gqhe,gkhe->ghqk", split(queries), split(key_rows)) * (1.0 / math.sqrt(HD))
    scores = jnp.where(allowed[:, None], scores, -1e30)
    attn_probs = jax.nn.softmax(scores, axis=-1)
    probs_low = attn_probs.astype(BF16)
    context = dot("ghqk,gkhe->gqhe", probs_low, split(value_rows)).astype(BF16)
    context = context.reshape(seqs * caps, features)
    attended = dot("ne,de->nd", context, full_proj)
    residual = picked + attended
    normed2, inverse2 = normalize(residual, gain2)
    norm_two = normed2.astype(BF16)
    mlp_out = 0.0
    grad_norm_two = 0.0
    grad_mlp = []
    for up, down in zip(full_up, full_down):
        hidden, slope = gelu_parts(dot("nd,df->nf", norm_two, up))
        mlp_out = mlp_out + dot("nf,df->nd", hidden, down)
        grad_pre = (dot("nd,df->nf", branch, down) * slope).astype(BF16)
        grad_norm_two = grad_norm_two + dot("nf,df->nd", grad_pre, up)
        grad_mlp += [
            dot("nd,nf->df", norm_two, grad_pre).astype(BF16),
            dot("nd,nf->df", branch, hidden).astype(BF16),
        ]
    delta = attended + mlp_out
    new_rows = (picked + gating * delta).astype(BF16)
    grad_score = jnp.sum(grad_rows * delta, axis=-1, keepdims=True) * gating * (1.0 - gating)
    grad_mid, grad_gain2 = norm_back(grad_norm_two, residual, inverse2, gain2)
    grad_attended = (grad_delta + grad_mid).astype(BF16)
    grad_proj = dot("nd,ne->de", grad_attended, context).astype(BF16)
    grad_context = split(dot("nd,de->ne", grad_attended, full_proj).astype(BF16))
    grad_probs = dot("gqhe,gkhe->ghqk", grad_context, split(value_rows))
    grad_scores = (
        attn_probs * (grad_probs - jnp.sum(attn_probs * grad_probs, axis=-1, keepdims=True))
    ).astype(BF16)
    join = lambda a: a.astype(BF16).reshape(seqs * caps, features)
    grad_values = join(dot("ghqk,gqhe->gkhe", probs_low, grad_context))
    grad_queries = join(
        dot("ghqk,gkhe->gqhe", grad_scores, split(key_rows)) * (1.0 / math.sqrt(HD))
    )
    grad_keys = join(dot("ghqk,gqhe->gkhe", grad_scores, split(queries)) * (1.0 / math.sqrt(HD)))
    grad_query = dot("nd,ne->de", norm_one, grad_queries).astype(BF16)
    grad_key = dot("nd,ne->de", norm_one, grad_keys).astype(BF16)
    grad_value = dot("nd,ne->de", norm_one, grad_values).astype(BF16)
    grad_norm_one = (
        dot("ne,de->nd", grad_queries, full_query)
        + dot("ne,de->nd", grad_keys, full_key)
        + dot("ne,de->nd", grad_values, full_value)
    )
    grad_picked_norm, grad_gain1 = norm_back(grad_norm_one, picked, inverse1, gain1)
    grad_router = jnp.sum(grad_score * picked, axis=0)
    grad_picked = (grad_rows + grad_mid + grad_picked_norm + grad_score * router).astype(BF16)

    small = jnp.stack([grad_router, grad_gain1, grad_gain2]).reshape(3, 1 << bits, rows)
    small = jnp.pad(small.transpose(1, 0, 2), ((0, 0), (0, 5), (0, 128 - rows)))
    grads = grad_mlp + [grad_proj, grad_query, grad_key, grad_value]
    summed, small = scatter_grads(bits, ranks, grads, small)
    out_up = jnp.concatenate(summed[0 : 2 * parts : 2], axis=1)
    out_down = jnp.concatenate(summed[1 : 2 * parts : 2], axis=1)
    out_proj, out_query, out_key, out_value = summed[2 * parts :]

    def put(base, new):
        placed = dot("scl,scd->sld", chosen, new.reshape(seqs, caps, features)).astype(BF16)
        routed = jnp.sum(chosen.astype(F32), axis=1) > 0
        return jnp.where(routed[:, :, None], placed, base)

    return (
        put(activations, new_rows),
        put(cotangent, grad_picked),
        small[0, :rows],
        small[1, :rows],
        small[2, :rows],
        out_query,
        out_key,
        out_value,
        out_proj,
        out_up,
        out_down,
    )


def solution(mesh):
    both = P(("dp", "tensor"), None, None)
    cut = P("dp", "tensor")
    one = P("dp")
    return jax.shard_map(
        shards,
        mesh=mesh,
        in_specs=(both, P("dp", None), one, one, one, one) + (cut,) * 6 + (both,),
        out_specs=(both, both, one, one, one) + (cut,) * 6,
        check_vma=False,
    )
```

time: 807 us -> 430 us (0.53)
  waiting for transfers between devices: 485 us -> 0 us
  Pallas kernels: 0 us -> 287 us
  blocking collectives: 102 us -> 0 us
  local copies, waits for them, and re-layouts: 102 us -> 40.3 us
  between operations: 17.1 us -> 1.7 us
  matrix products: 72.9 us -> 84.4 us
    reduce_scatter x10 -> x0, waiting for transfers between devices: 324 us -> none  [the longest x1 75.7 us: shards(): lax.psum_scatter(jnp.einsum('ncf,df->ncd', part_rows, full_up, preferred_...]
    pallas_call x0 -> x2, Pallas kernels: none -> 287 us  [the longest x1 152 us: scatter_grads(): pl.pallas_call(functools.partial(scatter_kernel, bits, ranks, chunks), ou...]
    all_gather x6 -> x0, waiting for transfers between devices: 160 us -> none  [the longest x1 47.1 us: shards(): lax.all_gather(grad_delta.astype(jnp.bfloat16), 'tensor', axis=0, tiled=T...]
    scatter x2 -> x0, local copies, waits for them, and re-layouts: 74 us -> none  [the longest x1 37.1 us: shards(): result = activations.at[seq_lines, own_routes].set(new_rows)]
    all_gather x7 -> x0, blocking collectives: 66.4 us -> none  [the longest x1 10.3 us: shards(): lax.all_gather(gain_attn, 'dp', axis=0, tiled=True)]
    unnamed x1 -> x0, blocking collectives: 24.8 us -> none
    reshape x0 -> x8, local copies, waits for them, and re-layouts: none -> 18 us  [shards(): split = lambda a: a.reshape(seqs, caps, heads, HD)]
    psum x1 -> x0, blocking collectives: 10.4 us -> none  [shards(): small = lax.psum((summed[6], summed[7], summed[8]), 'tensor')]
  transfers between devices with their start and end apart: 16 -> 0, of which waited for: 12 -> 0; matrix products, arithmetic and copies ran while one was open for 18% -> 0% of each run, Pallas kernels for 0% -> 0%
where the time goes in v1:
time: 430 us; the launch traced here: 423 us
  Pallas kernels  287 us (67%)
  matrix products  84.4 us (20%)
  local copies, waits for them, and re-layouts  40.3 us (9%)
  other arithmetic  9.53 us (2%)
    pallas_call x1, Pallas kernels, scatter_grads(): pl.pallas_call(functools.partial(scatter_kernel, bits, ranks, chunks), ou...  152 us
    pallas_call x1, Pallas kernels, gather_weights(): pl.pallas_call(functools.partial(gather_kernel, bits, ranks, chunks), out...  135 us
    dot_general x45, matrix products, dot(): return jnp.einsum(form, left, right, preferred_element_type=F32)  82.3 us
    reshape x8, local copies, waits for them, and re-layouts, shards(): split = lambda a: a.reshape(seqs, caps, heads, HD)  18 us
    unnamed x110, local copies, waits for them, and re-layouts  15.6 us

profile of v1, /device:TPU:0, one launch (start us, length us, event | category | flops | bytes accessed | tf_op | source)
XLA Modules:
  0.0 422.8 jit_solution(15943764452141430250)
XLA Ops:
  1.4 0.8 compare_and_fusion
  2.1 1.3 fusion.75.refs_12_
  3.8 1.9 fusion.80
  5.7 3.0 fusion.39
  8.6 134.8 %gather_weights.1 = (bf16[1024,1024]{1,0:T(8,128)(2,1)}, bf16[1024,1024]{1,0:T(8,128)(2,1)}, bf16[1024,1024]{1,0:T(8,128)(2,1)}, bf16[1024,1024]{1,0:T(8,128)(2,...) custom-call(bf16[128,256]{1,0:T(8,128)(2,1)} %refs_0_.1, ...), custom_call_target="tpu_custom_call" | custom-call | tf_op jit(solution)/shard_map/gather_weights/pallas_call | solution.py:219
  143.4 0.8 slice_bitcast_fusion
  144.2 3.3 multiply_reduce_fusion.6
  147.7 0.8 copy-done.47
  149.3 1.6 reshape.214
  150.9 2.0 copy.43
  152.9 2.7 convolution_convert_fusion.16
  155.6 1.5 convolution_convert_fusion.17
  157.1 2.7 reshape.212
  159.9 2.8 copy.44
  162.6 1.6 reshape.213
  164.3 2.0 copy.42
  166.3 2.2 fusion.83
  168.5 2.3 fusion.9
  171.4 0.9 multiply_reduce_fusion.4
  173.9 0.9 copy-done.11
  175.5 1.2 copy-done.12
  177.4 1.2 copy-done.19
  178.7 0.8 multiply_convert_fusion.5
  179.5 0.8 copy-done.36
  180.8 0.8 fusion.84
  181.7 0.8 convolution_add_fusion.7
  182.4 0.8 copy-done.24
  184.0 0.8 copy-done.40
  184.8 1.9 fusion.32
  186.8 1.0 fusion.5
  187.8 1.0 fusion.8
  188.8 13.3 %fusion.7 = bf16[256,1024]{1,0:T(8,128)(2,1)S(1)} fusion(bf16[256,1024]{1,0:T(8,128)(2,1)S(1)} %fusion.43, bf16[1024,1024]{1,0:T(8,128)(2,1)S(1)} %copy-done.24, f32[256,1024]{1,0:T(8,128)S(1)} %fusion.86), kind=kOutput, calls=%fused_computation.49 | convolution fusion | flops 539492352 | bytes 4194304 | tf_op jit(solution)/shard_map/nd,df->nf/dot_general | solution.py:515
  202.1 1.0 fusion.6
  203.8 0.8 convolution_add_fusion.4
  205.4 1.0 multiply_reduce_fusion.1
  207.4 0.8 copy-done.41
  208.2 1.5 convolution_convert_fusion.13
  209.7 2.5 reshape.215
  212.2 2.8 copy.49
  215.0 2.6 fusion.10
  218.8 2.2 convolution_convert_fusion.3.refs_8_
  221.0 2.2 convolution_convert_fusion.8.refs_3_
  223.1 2.2 convolution_convert_fusion.6.refs_5_
  225.3 2.1 convolution_convert_fusion.4.refs_7_
  227.5 2.1 convolution_convert_fusion.10.refs_1_
  231.3 0.8 fusion.11
  233.9 0.8 fusion.49
  235.5 0.8 convolution_add_fusion.1
  236.3 0.8 copy-done.39
  237.1 1.0 fusion.36
  238.9 0.8 fusion.31
  240.4 2.4 convolution_convert_fusion.refs_11_
  242.8 2.1 convolution_convert_fusion.1.refs_10_
  244.8 2.1 convolution_convert_fusion.2.refs_9_
  247.0 2.1 convolution_convert_fusion.5.refs_6_
  249.0 2.1 convolution_convert_fusion.7.refs_4_
  251.1 2.1 convolution_convert_fusion.9.refs_2_
  253.2 2.1 convolution_convert_fusion.11.refs_0_
  255.3 152.0 %scatter_grads.1 = (f32[128,256]{1,0:T(8,128)}, f32[128,256]{1,0:T(8,128)}, f32[128,256]{1,0:T(8,128)}, f32[128,256]{1,0:T(8,128)}, f32[128,256]{1,0:T(8,128)}, ...) custom-call(bf16[1024,1024]{1,0:T(8,128)(2,1)} %convolution_convert_, ...), custom_call_target="tpu_custom_call" | custom-call | tf_op jit(solution)/shard_map/scatter_grads/pallas_call | solution.py:452
  407.3 1.3 slice_bitcast_fusion.1
  408.6 1.9 pad_maximum_fusion
  410.6 1.9 pad_maximum_fusion.1
  412.5 4.5 %convert_select_fusion.1 = bf16[2,1024,1024]{2,1,0:T(8,128)(2,1)} fusion(bf16[2,1024,1024]{2,1,0:T(8,128)(2,1)} %param.13, pred[2,1024]{1,0:T(4,128)(4,1)S(1)} %broadcast_compare_fusion, bf16[2,128,1024]{2,1,0:T(8,128)(2,1)S(1)} %bitcast.197, s32[2,128]{1,0:T(2,128)S(1)} %get-tuple-element.74), kind=kOutput, calls=%fused_computation.2 | convolution fusion | flops 541327360 | bytes 8915968 | tf_op jit(solution)/shard_map/scl,scd->sld/dot_general | solution.py:515
  417.0 2.8 convert_select_fusion
  (133 shorter events, 19.2 us)
Async XLA Ops:
  144.2 4.3 %copy-start.21 = (bf16[1024,1024]{1,0:T(8,128)(2,1)S(1)}, bf16[1024,1024]{1,0:T(8,128)(2,1)}, u32[]{:S(2)}) copy-start(bf16[1024,1024]{1,0:T(8,128)(2,1)} %get-tuple-element.40) | copy-start | bytes 6291460
  147.7 0.8 copy-start.47
  152.9 13.4 %copy-start.28 = (bf16[2,128,16,64]{1,3,2,0:T(8,128)(2,1)}, bf16[2,128,16,64]{1,3,2,0:T(8,128)(2,1)S(1)}, u32[]{:S(2)}) copy-start(bf16[2,128,16,64]{1,3,2,0:T(8,128)(2,1)S(1)} %copy.43) | copy-start | bytes 1572868
  152.9 2.7 copy-start.38
  152.9 2.7 copy-start.48
  166.3 2.2 copy-start.34
  168.5 2.9 copy-start.17
  171.3 0.9 copy-start.14
  171.4 1.8 copy-start.13
  172.3 34.2 %copy-start = (f32[256,1024]{1,0:T(8,128)}, f32[256,1024]{1,0:T(8,128)S(1)}, u32[]{:S(2)}) copy-start(f32[256,1024]{1,0:T(8,128)S(1)} %get-tuple-element.72) | copy-start | bytes 3145732
  173.1 1.6 copy-start.11
  174.7 13.1 %copy-start.7 = (f32[256,1024]{1,0:T(8,128)}, f32[256,1024]{1,0:T(8,128)S(1)}, u32[]{:S(2)}) copy-start(f32[256,1024]{1,0:T(8,128)S(1)} %fusion.87) | copy-start | bytes 3145732
  174.7 2.0 copy-start.12
  176.7 12.1 %copy-start.3 = (f32[256,1024]{1,0:T(8,128)}, f32[256,1024]{1,0:T(8,128)S(1)}, u32[]{:S(2)}) copy-start(f32[256,1024]{1,0:T(8,128)S(1)} %fusion.86) | copy-start | bytes 3145732
  176.7 2.0 copy-start.19
  178.7 23.4 %copy-start.5 = (f32[256,1024]{1,0:T(8,128)}, f32[256,1024]{1,0:T(8,128)S(1)}, u32[]{:S(2)}) copy-start(f32[256,1024]{1,0:T(8,128)S(1)} %fusion.85) | copy-start | bytes 3145732
  178.7 2.2 copy-start.20
  179.5 0.8 copy-start.36
  179.5 2.1 copy-start.23
  181.6 1.6 copy-start.24
  183.2 1.6 copy-start.40
  187.8 15.2 %copy-start.26 = (bf16[256,1024]{1,0:T(8,128)(2,1)}, bf16[256,1024]{1,0:T(8,128)(2,1)S(1)}, u32[]{:S(2)}) copy-start(bf16[256,1024]{1,0:T(8,128)(2,1)S(1)} %fusion.5) | copy-start | bytes 1572868
  188.8 16.6 %copy-start.43 = (bf16[256,1024]{1,0:T(8,128)(2,1)}, bf16[256,1024]{1,0:T(8,128)(2,1)S(1)}, u32[]{:S(2)}) copy-start(bf16[256,1024]{1,0:T(8,128)(2,1)S(1)} %fusion.8) | copy-start | bytes 1572868
  202.1 2.5 copy-start.30
  203.1 1.5 copy-start.32
  206.4 1.0 copy-start.9
  207.4 0.8 copy-start.41
  217.6 1.0 copy-start.15
  217.6 1.2 copy-start.42
  218.2 2.8 copy-start.6
  221.0 2.2 copy-start.4
  223.1 2.2 copy-start.8
  225.3 2.1 copy-start.37
  227.4 2.1 copy-start.25
  227.4 2.1 copy-start.45
  227.4 2.2 copy-start.46
  230.2 1.0 copy-start.35
  231.3 1.0 copy-start.29
  232.3 1.6 copy-start.18
  233.9 1.6 copy-start.22
  235.5 1.6 copy-start.39
  237.1 1.2 copy-start.1
  237.1 1.5 copy-start.10
  237.1 1.9 copy-start.16
  244.8 2.1 copy-start.44
  247.0 2.1 copy-start.31
  249.0 2.1 copy-start.33
  251.1 2.1 copy-start.27
  412.5 4.5 %copy-start.2 = (bf16[2,1024,1024]{2,1,0:T(8,128)(2,1)S(1)}, bf16[2,1024,1024]{2,1,0:T(8,128)(2,1)}, u32[]{:S(2)}) copy-start(bf16[2,1024,1024]{2,1,0:T(8,128)(2,1)} %param.25) | copy-start | bytes 12582916
  417.0 2.8 copy-start.52
  417.0 3.5 copy-start.51
  417.0 4.1 copy-start.50
  417.0 4.8 %copy-start.49 = (f32[128,256]{1,0:T(8,128)S(1)}, f32[128,256]{1,0:T(8,128)}, u32[]{:S(2)}) copy-start(f32[128,256]{1,0:T(8,128)} %get-tuple-element.132) | copy-start | bytes 393220

commit v2 on v0

v2 whole, which is shorter than its diff:
```python
import functools
import math

import jax
import jax.numpy as jnp
from jax import lax
from jax.experimental import pallas as pl
from jax.experimental.pallas import tpu as pltpu
from jax.sharding import PartitionSpec as P

HD = 64
PIC = 256
AHEAD = 2
RING = 8
PAUSE = 2
MESH = pl.DeviceIdType.MESH
ANY = pl.BlockSpec(memory_space=pl.ANY)
VMEM = pl.BlockSpec(memory_space=pltpu.VMEM)
BF16 = jnp.bfloat16
F32 = jnp.float32

inv_root_two = 0.7071067811865476
inv_root_two_pi = 0.3989422804014327


def bit_of(value, bit):
    return lax.rem(lax.div(value, 1 << bit), 2)


def flipped(value, bit):
    return value + (1 - 2 * bit_of(value, bit)) * (1 << bit)


def cleared(value, bits):
    for bit in bits:
        value = value - bit_of(value, bit) * (1 << bit)
    return value


def spread(step, bits):
    value = 0
    for place, bit in enumerate(bits):
        value = value + lax.rem(lax.div(step, 1 << place), 2) * (1 << bit)
    return value


def each(count, body):
    if count <= 4:
        for step in range(count):
            body(jnp.int32(step))
    else:
        lax.fori_loop(0, count, lambda step, _: body(step), None)


def repeat(count, body):
    def step(index, _):
        body(index)

    lax.fori_loop(0, count, step, None)


def span(index, size):
    return pl.ds(pl.multiple_of(index * size, size), size)


def orders(bits):
    return (tuple(range(bits - 1, 0, -1)), tuple(range(1, bits)))


def remote(src, dst, send, recv, where):
    return pltpu.make_async_remote_copy(
        src_ref=src, dst_ref=dst, send_sem=send, recv_sem=recv, device_id=where, device_id_type=MESH
    )


def contract(left, right, axis_left, axis_right):
    return lax.dot_general(
        left, right, (((axis_left,), (axis_right,)), ((), ())), preferred_element_type=F32
    )


def layer_kernel(
    bits,
    ranks,
    chunks,
    shards,
    vec,
    picked,
    grad_rows,
    allowed,
    sums,
    vec_sum,
    new_rows,
    new_grads,
    held,
    from_core,
    from_z,
    vecs,
    grad_vecs,
    vec_path,
    vec_z,
    params,
    gates,
    scores_of,
    norm_one,
    qkv,
    context,
    attended,
    norm_two,
    norm_two_t,
    branch,
    branch_t,
    hidden,
    grad_pre,
    mlp,
    grad_two,
    send_z,
    recv_z,
    send_p,
    recv_p,
    send_c,
    recv_c,
    send_v,
    recv_v,
    local,
    out_c,
    in_c,
    out_p,
    in_p,
    out_z,
    in_z,
    out_v,
    in_v,
    *from_path,
):
    me, rank = lax.axis_index("dp"), lax.axis_index("tensor")
    _, rows, width = shards.shape
    count, full = picked.shape
    seqs, caps, _ = allowed.shape
    half = full // 2
    seat, pair = bit_of(me, 0), lax.div(me, 2)
    pairs = 1 << (bits - 1)
    paths = orders(bits)
    back_paths = tuple(tuple(bit - 1 for bit in order[::-1]) for order in paths)
    tile = 32
    block = 256
    blocks = full // block

    barrier = pltpu.get_barrier_semaphore()
    for bit in range(bits):
        pl.semaphore_signal(barrier, 1, device_id=(flipped(me, bit), rank), device_id_type=MESH)
    for hop in range(1, ranks):
        pl.semaphore_signal(
            barrier, 1, device_id=(me, lax.rem(rank + hop, ranks)), device_id_type=MESH
        )
    pl.semaphore_wait(barrier, bits + ranks - 1)

    mine = span(me, rows)
    columns = span(rank, width)

    def keep_own(chunk):
        return pltpu.make_async_copy(
            shards.at[chunk], held.at[chunk, mine, columns], local.at[chunk]
        )

    def bulk(chunk, depth, breadth):
        return held.at[chunk, pl.ds(0, depth), pl.ds(0, breadth)]

    def z_copy(chunk):
        part = bulk(chunk, rows, width * (ranks - 1))
        return remote(part, part, send_z.at[chunk], recv_z.at[chunk], (me, rank))

    def send_path(chunk, colour, stage):
        order = paths[colour]
        other = (flipped(me, order[stage]), rank)

        def send(step):
            index = cleared(me, order[:stage]) + spread(step, order[:stage])
            part = held.at[chunk, span(index, rows), pl.ds(colour * half, half)]
            remote(
                part,
                part,
                send_p.at[chunk, colour, stage],
                recv_p.at[chunk, colour, stage],
                other,
            ).start()

        each(1 << stage, send)

    def path_copy(chunk, colour, stage):
        part = bulk(chunk, rows << stage, half)
        return remote(
            part,
            part,
            send_p.at[chunk, colour, stage],
            recv_p.at[chunk, colour, stage],
            (me, rank),
        )

    def send_core(chunk):
        other = (flipped(me, 0), rank)

        def send(step):
            part = held.at[chunk, span(2 * step + seat, rows)]
            remote(part, part, send_c.at[chunk], recv_c.at[chunk], other).start()

        each(pairs, send)

    def core_copy(chunk):
        part = bulk(chunk, rows << (bits - 1), full)
        return remote(part, part, send_c.at[chunk], recv_c.at[chunk], (me, rank))

    def all_sent(chunk):
        for colour in range(2):
            for stage in range(bits - 1):
                path_copy(chunk, colour, stage).wait_send()
        core_copy(chunk).wait_send()

    def gather_stage(chunk, stage):
        if stage == 0:
            keep_own(chunk).wait()
            z_copy(chunk).wait_recv()
        elif stage < bits:
            for colour in range(2):
                path_copy(chunk, colour, stage - 1).wait_recv()
        else:
            core_copy(chunk).wait_recv()
        if stage < bits - 1:
            for colour in range(2):
                send_path(chunk, colour, stage)
        elif stage == bits - 1:
            send_core(chunk)

    def turn(item):
        return jnp.where(item < chunks - 4, item, item - PAUSE)

    def slot(item):
        return jnp.where(item < chunks - 4, item + 4, item - PAUSE - chunks + 4)

    def give_core(item):
        def send(step):
            remote(
                held.at[slot(item), span(2 * step + 1 - seat, rows)],
                from_core.at[lax.rem(turn(item), RING), step],
                out_c.at[turn(item)],
                in_c.at[turn(item)],
                (flipped(me, 0), rank),
            ).start()

        each(pairs, send)

    def given_core(item):
        part = from_core.at[lax.rem(turn(item), RING)]
        return remote(part, part, out_c.at[turn(item)], in_c.at[turn(item)], (me, rank))

    def add_to(item, index, where, source):
        step = min(rows, tile)
        for start in range(0, rows, step):
            place = pl.ds(pl.multiple_of((2 * index + seat) * rows, rows) + start, step)
            here = held.at[slot(item), place, where]
            here[...] = (
                here[...].astype(F32) + source[pl.ds(start, step)].astype(F32)
            ).astype(BF16)

    def add_core(item):
        repeat(
            pairs,
            lambda step: add_to(
                item, step, pl.ds(0, full), from_core.at[lax.rem(turn(item), RING), step]
            ),
        )

    def members(stage, order, step, kept):
        bit, later = order[stage], order[stage + 1 :]
        index = pair if kept else flipped(pair, bit)
        return cleared(index, later) + spread(step, later)

    def give_path(item, colour, stage):
        order = back_paths[colour]
        other = (2 * flipped(pair, order[stage]) + seat, rank)

        def send(step):
            index = members(stage, order, step, False)
            remote(
                held.at[
                    slot(item), span(2 * index + seat, rows), pl.ds(colour * half, half)
                ],
                from_path[stage].at[turn(item), colour, step],
                out_p.at[turn(item), colour, stage],
                in_p.at[turn(item), colour, stage],
                other,
            ).start()

        each(1 << (len(order) - stage - 1), send)

    def given_path(item, colour, stage):
        part = from_path[stage].at[turn(item), colour]
        return remote(
            part,
            part,
            out_p.at[turn(item), colour, stage],
            in_p.at[turn(item), colour, stage],
            (me, rank),
        )

    def add_path(item, colour, stage):
        order = back_paths[colour]
        repeat(
            1 << (len(order) - stage - 1),
            lambda step: add_to(
                item,
                members(stage, order, step, True),
                pl.ds(colour * half, half),
                from_path[stage].at[turn(item), colour, step],
            ),
        )

    def give_across(item):
        for hop in range(1, ranks):
            to = lax.rem(rank + hop, ranks)
            remote(
                held.at[slot(item), mine, span(to, width)],
                from_z.at[turn(item), hop - 1],
                out_z.at[turn(item)],
                in_z.at[turn(item)],
                (me, to),
            ).start()

    def given_across(item):
        part = from_z.at[turn(item)]
        return remote(part, part, out_z.at[turn(item)], in_z.at[turn(item)], (me, rank))

    def finish(item):
        total = held[slot(item), mine, columns].astype(F32)
        for hop in range(1, ranks):
            total = total + from_z[turn(item), hop - 1].astype(F32)
        sums[slot(item)] = total

    def scatter_stage(item, stage):
        if stage == 1:
            given_core(item).wait_recv()
            add_core(item)
        elif 1 < stage <= bits:
            for colour in range(2):
                given_path(item, colour, stage - 2).wait_recv()
                add_path(item, colour, stage - 2)
        elif stage == bits + 1:
            given_across(item).wait_recv()
            finish(item)
        if stage == 0:
            give_core(item)
        elif stage < bits:
            for colour in range(2):
                give_path(item, colour, stage - 1)
        elif stage == bits:
            give_across(item)

    def vec_gather():
        path = tuple(range(bits - 1, -1, -1))
        for stage, bit in enumerate(path):
            other = (flipped(me, bit), rank)

            def send(step, stage=stage, other=other):
                index = cleared(me, path[:stage]) + spread(step, path[:stage])
                remote(
                    vecs.at[index], vecs.at[index], send_v.at[stage], recv_v.at[stage], other
                ).start()

            each(1 << stage, send)
            part = vecs.at[pl.ds(0, 1 << stage)]
            remote(part, part, send_v.at[stage], recv_v.at[stage], other).wait()
        params[...] = jnp.zeros_like(params)
        lane = lax.broadcasted_iota(jnp.int32, (128, full), 0)
        column = lax.broadcasted_iota(jnp.int32, (128, full), 1)

        def place(index):
            chosen = ((lane < rows) & (column == index * rows + lane)).astype(F32).astype(BF16)
            params[...] += contract(vecs[index].astype(BF16), chosen, 1, 0)

        repeat(1 << bits, place)

    vec_path_of = tuple(range(bits))

    def vec_stage(stage):
        if stage > 0:
            earlier = vec_path_of[stage:]
            amount = 1 << len(earlier)
            part = vec_path.at[pl.ds(amount - 1, amount)]
            remote(part, part, out_v.at[stage - 1], in_v.at[stage - 1], (me, rank)).wait()

            def add(step):
                index = cleared(me, earlier) + spread(step, earlier)
                grad_vecs[index] = grad_vecs[index] + vec_path[amount - 1 + step]

            repeat(amount, add)
        if stage < bits:
            bit, later = vec_path_of[stage], vec_path_of[stage + 1 :]
            amount = 1 << len(later)

            def send(step):
                index = cleared(flipped(me, bit), later) + spread(step, later)
                remote(
                    grad_vecs.at[index],
                    vec_path.at[amount - 1 + step],
                    out_v.at[stage],
                    in_v.at[stage],
                    (flipped(me, bit), rank),
                ).start()

            each(amount, send)
        else:
            for hop in range(1, ranks):
                to = (me, lax.rem(rank + hop, ranks))
                remote(
                    grad_vecs.at[me], vec_z.at[hop - 1], out_v.at[bits], in_v.at[bits], to
                ).start()

    def vec_finish():
        remote(vec_z, vec_z, out_v.at[bits], in_v.at[bits], (me, rank)).wait()
        total = grad_vecs[me]
        for hop in range(1, ranks):
            total = total + vec_z[hop - 1]
        vec_sum[...] = total

    def router():
        return params[0:1, :]

    def gain_one():
        return params[1:2, :]

    def gain_two():
        return params[2:3, :]

    def by_rows(body):
        repeat(count // tile, lambda index: body(span(index, tile)))

    def by_blocks(body):
        repeat(blocks, lambda index: body(span(index, block)))

    def inverse_of(values):
        return lax.rsqrt(jnp.mean(values * values, axis=-1, keepdims=True) + 1e-06)

    def wide(values):
        return jnp.broadcast_to(values, (values.shape[0], 128))

    def transpose_to(target, source):
        for start in range(0, full, 128):
            part = source[:, start : start + 128].astype(F32)
            target[start : start + 128, :] = part.T.astype(BF16)

    def prepare():
        def body(part):
            values = picked[part].astype(F32)
            logit = jnp.sum(values * router(), axis=-1, keepdims=True)
            gate = 1.0 / (1.0 + jnp.exp(-logit))
            gates[part] = wide(gate)
            norm_one[part] = (values * inverse_of(values) * gain_one()).astype(BF16)
            branch[part] = (gate * grad_rows[part].astype(F32)).astype(BF16)

        by_rows(body)
        transpose_to(branch_t, branch)

    def project(which):
        def body(part):
            qkv[which, :, part] = contract(norm_one[...], held[which, :, part], 1, 0).astype(BF16)

        by_blocks(body)

    lanes = lax.broadcasted_iota(jnp.int32, (1, 2 * HD), 1)

    def own_lanes(values, head):
        inside = (lanes < HD) if head == 0 else (lanes >= HD)
        return jnp.where(inside, values, jnp.zeros_like(values))

    def probabilities(seq, queries, keys, head):
        scores = contract(own_lanes(queries, head), keys, 1, 1) * (1.0 / math.sqrt(HD))
        scores = jnp.where(allowed[seq] > 0, scores, -1e30)
        powers = jnp.exp(scores - jnp.max(scores, axis=-1, keepdims=True))
        return powers / jnp.sum(powers, axis=-1, keepdims=True)

    def attend():
        def body(index):
            part = span(index, 2 * HD)
            for seq in range(seqs):
                place = pl.ds(seq * caps, caps)
                queries, keys = qkv[0, place, part], qkv[1, place, part]
                values = qkv[2, place, part]
                total = 0.0
                for head in range(2):
                    probs = probabilities(seq, queries, keys, head).astype(BF16)
                    total = total + contract(probs, own_lanes(values, head), 1, 0)
                context[place, part] = total.astype(BF16)

        repeat(full // (2 * HD), body)

    def leave_attention():
        def body(part):
            attended[:, part] = contract(context[...], held[3, part, :], 1, 1)

        by_blocks(body)

        def rest(part):
            values = picked[part].astype(F32) + attended[part]
            norm_two[part] = (values * inverse_of(values) * gain_two()).astype(BF16)
            mlp[part] = jnp.zeros((tile, full), F32)
            grad_two[part] = jnp.zeros((tile, full), F32)

        by_rows(rest)
        transpose_to(norm_two_t, norm_two)

    def feed_forward(up, down):
        def units(part):
            pre = contract(norm_two[...], held[up, :, part], 1, 0)
            bell = 0.5 * (1.0 + lax.erf(pre * inv_root_two))
            slope = bell + pre * jnp.exp(-0.5 * pre * pre) * inv_root_two_pi
            hidden[:, part] = (pre * bell).astype(BF16)
            grad_hidden = contract(branch[...], held[down, :, part], 1, 0)
            grad_pre[:, part] = (grad_hidden * slope).astype(BF16)

        by_blocks(units)

        def outputs(part):
            mlp[:, part] += contract(hidden[...], held[down, part, :], 1, 1)
            grad_two[:, part] += contract(grad_pre[...], held[up, part, :], 1, 1)

        by_blocks(outputs)
        all_sent(up)
        all_sent(down)

        def gradients(part):
            held[down, :, part] = contract(branch_t[...], hidden[:, part], 1, 0).astype(BF16)
            held[up, :, part] = contract(norm_two_t[...], grad_pre[:, part], 1, 0).astype(BF16)

        by_blocks(gradients)

    small = params

    def enter_back():
        grad_attended, grad_attended_t, grad_context = norm_two, norm_two_t, hidden
        small[3:6, :] = jnp.zeros((3, full), F32)

        def body(part):
            values = picked[part].astype(F32)
            gate = gates[part, 0:1]
            delta = attended[part] + mlp[part]
            new_rows[part] = (values + gate * delta).astype(BF16)
            rows_in = grad_rows[part].astype(F32)
            score = jnp.sum(rows_in * delta, axis=-1, keepdims=True) * gate * (1.0 - gate)
            scores_of[part] = wide(score)
            small[3:4, :] += jnp.sum(score * values, axis=0, keepdims=True)
            residual = values + attended[part]
            inverse = inverse_of(residual)
            grad = grad_two[part]
            small[5:6, :] += jnp.sum(grad * residual * inverse, axis=0, keepdims=True)
            scaled = grad * gain_two()
            mean = jnp.mean(scaled * residual, axis=-1, keepdims=True)
            grad_mid = inverse * scaled - residual * (inverse * inverse * inverse * mean)
            grad_two[part] = grad_mid
            grad_attended[part] = (gate * rows_in + grad_mid).astype(BF16)

        by_rows(body)
        transpose_to(grad_attended_t, grad_attended)

        def through(part):
            grad_context[:, part] = contract(grad_attended[...], held[3, :, part], 1, 0).astype(BF16)

        by_blocks(through)
        for chunk in range(4):
            all_sent(chunk)

        def weights(part):
            held[3, :, part] = contract(grad_attended_t[...], context[:, part], 1, 0).astype(BF16)

        by_blocks(weights)

    def attend_back():
        grad_context = hidden
        grads = (branch, grad_pre, context)

        def body(index):
            part = span(index, 2 * HD)
            for seq in range(seqs):
                place = pl.ds(seq * caps, caps)
                queries, keys = qkv[0, place, part], qkv[1, place, part]
                values, grad = qkv[2, place, part], grad_context[place, part]
                grad_q, grad_k, grad_v = 0.0, 0.0, 0.0
                for head in range(2):
                    probs = probabilities(seq, queries, keys, head)
                    grad_probs = contract(own_lanes(grad, head), values, 1, 1)
                    inner = jnp.sum(probs * grad_probs, axis=-1, keepdims=True)
                    grad_scores = (probs * (grad_probs - inner)).astype(BF16)
                    low = probs.astype(BF16)
                    grad_v = grad_v + contract(low, own_lanes(grad, head), 0, 0)
                    grad_q = grad_q + contract(grad_scores, own_lanes(keys, head), 1, 0)
                    grad_k = grad_k + contract(grad_scores, own_lanes(queries, head), 0, 0)
                scale = 1.0 / math.sqrt(HD)
                grads[0][place, part] = (grad_q * scale).astype(BF16)
                grads[1][place, part] = (grad_k * scale).astype(BF16)
                grads[2][place, part] = grad_v.astype(BF16)

        repeat(full // (2 * HD), body)

    def leave_back():
        grads = (branch, grad_pre, context)
        grad_one, norm_one_t = mlp, branch_t

        def through(part):
            total = contract(grads[0][...], held[0, part, :], 1, 1)
            for which in (1, 2):
                total = total + contract(grads[which][...], held[which, part, :], 1, 1)
            grad_one[:, part] = total

        by_blocks(through)
        transpose_to(norm_one_t, norm_one)

        def weights(part):
            for which in range(3):
                held[which, :, part] = contract(norm_one_t[...], grads[which][:, part], 1, 0).astype(
                    BF16
                )

        by_blocks(weights)

        def body(part):
            values = picked[part].astype(F32)
            inverse = inverse_of(values)
            grad = grad_one[part]
            small[4:5, :] += jnp.sum(grad * values * inverse, axis=0, keepdims=True)
            scaled = grad * gain_one()
            mean = jnp.mean(scaled * values, axis=-1, keepdims=True)
            grad_norm = inverse * scaled - values * (inverse * inverse * inverse * mean)
            score = scores_of[part, 0:1]
            total = grad_rows[part].astype(F32) + grad_two[part] + grad_norm + score * router()
            new_grads[part] = total.astype(BF16)

        by_rows(body)
        own = small[...]
        if rows == 128:
            for index in range(1 << bits):
                grad_vecs[index] = own[:, index * rows : (index + 1) * rows]
        else:
            column = lax.broadcasted_iota(jnp.int32, (full, 128), 0)
            lane = lax.broadcasted_iota(jnp.int32, (full, 128), 1)

            def place(index):
                chosen = ((lane < rows) & (column == index * rows + lane)).astype(F32)
                grad_vecs[index] = jnp.dot(
                    own, chosen, precision=lax.Precision.HIGHEST, preferred_element_type=F32
                )

            repeat(1 << bits, place)

    def start(chunk):
        keep_own(chunk).start()
        for hop in range(1, ranks):
            remote(
                shards.at[chunk],
                held.at[chunk, mine, columns],
                send_z.at[chunk],
                recv_z.at[chunk],
                (me, lax.rem(rank + hop, ranks)),
            ).start()

    keep_vec = pltpu.make_async_copy(vec, vecs.at[me], local.at[chunks])
    keep_vec.start()
    repeat(chunks, start)
    keep_vec.wait()
    vec_gather()
    prepare()
    lead = AHEAD * bits
    first = lead + 5
    items = chunks + PAUSE
    vec_first = lead + chunks + PAUSE + 1

    def tick(now, _):
        for stage in range(bits, -1, -1):
            chunk = now - AHEAD * stage

            @pl.when((chunk >= 0) & (chunk < chunks))
            def _(chunk=chunk, stage=stage):
                gather_stage(chunk, stage)

        whole = now - lead
        pl.when((whole >= 0) & (whole < 3))(lambda: project(whole))
        pl.when(whole == 2)(attend)
        pl.when(whole == 3)(leave_attention)
        pl.when((whole >= 5) & (whole < chunks) & (lax.rem(whole, 2) == 1))(
            lambda: feed_forward(whole - 1, whole)
        )
        for stage in range(bits + 1, -1, -1):
            item = now - first - AHEAD * stage
            inside = (item >= 0) & (item < items)
            paused = (item >= chunks - 4) & (item < chunks - 4 + PAUSE)

            @pl.when(inside & jnp.logical_not(paused))
            def _(item=item, stage=stage):
                scatter_stage(item, stage)

        pl.when(whole == chunks)(enter_back)
        pl.when(whole == chunks + 1)(attend_back)
        pl.when(whole == chunks + 2)(leave_back)
        for stage in range(bits + 1):
            pl.when(now == vec_first + AHEAD * stage)(functools.partial(vec_stage, stage))
        pl.when(now == vec_first + AHEAD * (bits + 1))(vec_finish)

    last = max(first + items - 1 + AHEAD * (bits + 1), vec_first + AHEAD * (bits + 1))
    lax.fori_loop(0, last + 1, tick, None)

    def drain(chunk):
        z_copy(chunk).wait_send()
        item = jnp.where(chunk < chunks - 4, chunk, chunk + PAUSE)
        given_core(item).wait_send()
        for colour in range(2):
            for stage in range(bits - 1):
                given_path(item, colour, stage).wait_send()
        given_across(item).wait_send()

    repeat(chunks, drain)


def run_layer(bits, ranks, shards, vec, picked, grad_rows, allowed):
    chunks, rows, width = shards.shape
    depth, breadth, pairs = rows << bits, width * ranks, 1 << (bits - 1)
    count, full = picked.shape
    dma = pltpu.SemaphoreType.DMA
    low = pltpu.VMEM((count, full), BF16)
    turned = pltpu.VMEM((full, count), BF16)
    high = pltpu.VMEM((count, full), F32)
    return pl.pallas_call(
        functools.partial(layer_kernel, bits, ranks, chunks),
        out_shape=[
            jax.ShapeDtypeStruct((chunks, rows, width), F32),
            jax.ShapeDtypeStruct((8, 128), F32),
            jax.ShapeDtypeStruct((count, full), BF16),
            jax.ShapeDtypeStruct((count, full), BF16),
        ],
        in_specs=[ANY] + [VMEM] * 4,
        out_specs=[VMEM] * 4,
        scratch_shapes=[
            pltpu.VMEM((chunks, depth, breadth), BF16),
            pltpu.VMEM((RING, pairs, rows, breadth), BF16),
            pltpu.VMEM((chunks, ranks - 1, rows, width), BF16),
            pltpu.VMEM((1 << bits, 8, 128), F32),
            pltpu.VMEM((1 << bits, 8, 128), F32),
            pltpu.VMEM((1 << bits, 8, 128), F32),
            pltpu.VMEM((ranks - 1, 8, 128), F32),
            pltpu.VMEM((8, full), F32),
            pltpu.VMEM((count, 128), F32),
            pltpu.VMEM((count, 128), F32),
            low,
            pltpu.VMEM((3, count, full), BF16),
            low,
            high,
            low,
            turned,
            low,
            turned,
            low,
            low,
            high,
            high,
            dma((chunks,)),
            dma((chunks,)),
            dma((chunks, 2, bits - 1)),
            dma((chunks, 2, bits - 1)),
            dma((chunks,)),
            dma((chunks,)),
            dma((bits,)),
            dma((bits,)),
            dma((chunks + 1,)),
            dma((chunks,)),
            dma((chunks,)),
            dma((chunks, 2, bits - 1)),
            dma((chunks, 2, bits - 1)),
            dma((chunks,)),
            dma((chunks,)),
            dma((bits + 1,)),
            dma((bits + 1,)),
            *[
                pltpu.VMEM((chunks, 2, pairs >> (stage + 1), rows, breadth // 2), BF16)
                for stage in range(bits - 1)
            ],
        ],
        compiler_params=pltpu.CompilerParams(
            collective_id=1, has_side_effects=True, vmem_limit_bytes=67043328
        ),
        name="layer_kernel",
    )(shards, vec, picked, grad_rows, allowed)


def span_mask(positions, starts):
    later = positions[:, None, :] <= positions[:, :, None]
    begin = starts[:, None]
    inside = (positions >= begin) & (positions < begin + PIC)
    return later | inside[:, :, None] & inside[:, None, :]


def dot(form, left, right):
    return jnp.einsum(form, left, right, preferred_element_type=F32)


def shards(
    activations,
    routes,
    pic_start,
    router_w,
    gain_attn,
    gain_mlp,
    w_query,
    w_key,
    w_value,
    w_proj,
    w_up,
    w_down,
    cotangent,
):
    seqs, length, features = activations.shape
    ranks = lax.axis_size("tensor")
    bits = lax.axis_size("dp").bit_length() - 1
    rank = lax.axis_index("tensor")
    rows, width = w_query.shape
    parts = w_up.shape[1] // width
    own_routes = lax.dynamic_slice_in_dim(routes, rank * seqs, seqs, 0)
    own_start = lax.dynamic_slice_in_dim(pic_start, rank * seqs, seqs, 0)
    caps = routes.shape[1]

    vec = jnp.stack([router_w, gain_attn, gain_mlp]).astype(F32)
    vec = jnp.pad(vec, ((0, 5), (0, 128 - rows)))
    pieces = [w_query, w_key, w_value, w_proj]
    for part in range(parts):
        columns = slice(part * width, (part + 1) * width)
        pieces += [w_up[:, columns], w_down[:, columns]]
    chosen = (own_routes[:, :, None] == jnp.arange(length)[None, None, :]).astype(BF16)
    picked = dot("scl,sld->scd", chosen, activations).astype(BF16)
    grad_rows = dot("scl,sld->scd", chosen, cotangent).astype(BF16)
    sums, small, new_rows, new_grads = run_layer(
        bits,
        ranks,
        jnp.stack(pieces),
        vec,
        picked.reshape(seqs * caps, features),
        grad_rows.reshape(seqs * caps, features),
        span_mask(own_routes, own_start).astype(F32),
    )

    def put(base, new):
        placed = dot("scl,scd->sld", chosen, new.reshape(seqs, caps, features)).astype(BF16)
        routed = jnp.sum(chosen.astype(F32), axis=1) > 0
        return jnp.where(routed[:, :, None], placed, base)

    def side_by_side(first):
        return jnp.concatenate([sums[first + 2 * part] for part in range(parts)], axis=1)

    return (
        put(activations, new_rows),
        put(cotangent, new_grads),
        small[3, :rows],
        small[4, :rows],
        small[5, :rows],
        sums[0],
        sums[1],
        sums[2],
        sums[3],
        side_by_side(4),
        side_by_side(5),
    )


def solution(mesh):
    both = P(("dp", "tensor"), None, None)
    cut = P("dp", "tensor")
    one = P("dp")
    return jax.shard_map(
        shards,
        mesh=mesh,
        in_specs=(both, P("dp", None), one, one, one, one) + (cut,) * 6 + (both,),
        out_specs=(both, both, one, one, one) + (cut,) * 6,
        check_vma=False,
    )
```

time: 807 us -> 265 us (0.33); the launches traced: 795 us -> 265 us
  waiting for transfers between devices: 485 us -> 0 us
  Pallas kernels: 0 us -> 235 us
  blocking collectives: 102 us -> 0 us
  local copies, waits for them, and re-layouts: 102 us -> 12.3 us
  matrix products: 72.9 us -> 11.1 us
  between operations: 17.1 us -> 0.75 us
  other arithmetic: 15.3 us -> 5.86 us
    reduce_scatter x10 -> x0, waiting for transfers between devices: 324 us -> none  [the longest x1 75.7 us: shards(): lax.psum_scatter(jnp.einsum('ncf,df->ncd', part_rows, full_up, preferred_...]
    pallas_call x0 -> x1, Pallas kernels: none -> 235 us  [run_layer(): pl.pallas_call(functools.partial(layer_kernel, bits, ranks, chunks), out_...]
    all_gather x6 -> x0, waiting for transfers between devices: 160 us -> none  [the longest x1 47.1 us: shards(): lax.all_gather(grad_delta.astype(jnp.bfloat16), 'tensor', axis=0, tiled=T...]
    scatter x2 -> x0, local copies, waits for them, and re-layouts: 74 us -> none  [the longest x1 37.1 us: shards(): result = activations.at[seq_lines, own_routes].set(new_rows)]
    all_gather x7 -> x0, blocking collectives: 66.4 us -> none  [the longest x1 10.3 us: shards(): lax.all_gather(gain_attn, 'dp', axis=0, tiled=True)]
    dot_general x26 -> x4, matrix products: 72.9 us -> 11.1 us  [dot(): return jnp.einsum(form, left, right, preferred_element_type=F32)]
    unnamed x1 -> x0, blocking collectives: 24.8 us -> none
    psum x1 -> x0, blocking collectives: 10.4 us -> none  [shards(): small = lax.psum((summed[6], summed[7], summed[8]), 'tensor')]
  transfers between devices with their start and end apart: 16 -> 0, of which waited for: 12 -> 0; matrix products, arithmetic and copies ran while one was open for 18% -> 0% of each run, Pallas kernels for 0% -> 0%
where the time goes in v2:
time: 265 us
  Pallas kernels  235 us (89%)
  local copies, waits for them, and re-layouts  12.3 us (5%)
  matrix products  11.1 us (4%)
  other arithmetic  5.86 us (2%)
    pallas_call x1, Pallas kernels, run_layer(): pl.pallas_call(functools.partial(layer_kernel, bits, ranks, chunks), out_...  235 us
    dot_general x4, matrix products, dot(): return jnp.einsum(form, left, right, preferred_element_type=F32)  11.1 us
    unnamed x39, local copies, waits for them, and re-layouts  7.98 us

profile of v2, /device:TPU:0, one launch (start us, length us, event | category | flops | bytes accessed | tf_op | source)
XLA Modules:
  0.0 265.1 jit_solution(18079022019311174868)
XLA Ops:
  0.6 0.0 copy-start
  0.7 0.9 broadcast_add_fusion
  1.5 1.0 compare_and_fusion
  2.5 0.0 copy-start.7
  2.5 1.3 fusion.10.vec
  3.8 0.2 convert_reduce_fusion
  4.0 0.6 broadcast_compare_fusion
  4.6 0.8 or_convert_fusion.allowed
  5.4 0.0 copy-start.10
  5.4 0.0 copy-start.11
  5.4 0.0 copy-start.12
  5.4 0.0 copy-start.13
  5.4 3.8 %convolution_convert_fusion.1 = bf16[2,128,1024]{2,1,0:T(8,128)(2,1)} fusion(bf16[2,1024,1024]{2,1,0:T(8,128)(2,1)} %param.13, s32[2,128]{1,0:T(2,128)S(1)} %get-tuple-element.20), kind=kOutput, calls=%fused_computation.3 | convolution fusion | flops 537395200 | bytes 4719616 | tf_op jit(solution)/shard_map/scl,sld->scd/dot_general | solution.py:799
  9.3 0.0 copy-start.5
  9.3 0.0 copy-start.6
  9.3 0.0 copy-done
  9.3 1.6 convolution_convert_fusion
  10.9 0.0 copy-done.7
  10.9 0.0 copy-done.10
  10.9 0.6 bitcast_dynamic-update-slice_fusion.11
  11.5 0.0 copy-done.11
  11.5 0.6 bitcast_dynamic-update-slice_fusion.10
  12.2 0.0 copy-done.12
  12.2 0.6 bitcast_dynamic-update-slice_fusion.9
  12.8 0.0 copy-done.13
  12.8 0.6 bitcast_dynamic-update-slice_fusion.8
  13.4 0.0 copy-done.5
  13.4 0.6 bitcast_dynamic-update-slice_fusion.7
  14.1 0.0 copy-done.6
  14.1 0.6 bitcast_dynamic-update-slice_fusion.6
  14.7 0.6 bitcast_dynamic-update-slice_fusion.5
  15.4 0.6 bitcast_dynamic-update-slice_fusion.4
  16.0 0.6 bitcast_dynamic-update-slice_fusion.3
  16.6 0.6 bitcast_dynamic-update-slice_fusion.2
  17.3 0.6 bitcast_dynamic-update-slice_fusion.1
  17.9 0.6 bitcast_dynamic-update-slice_fusion.shards
  18.5 235.2 %layer_kernel.1 = (f32[12,128,256]{2,1,0:T(8,128)}, f32[8,128]{1,0:T(8,128)}, bf16[256,1024]{1,0:T(8,128)(2,1)}, bf16[256,1024]{1,0:T(8,128)(2,1)}) custom-call(bf16[12,128,256]{2,1,0:T(8,128)(2,1)} %bitcast_dynamic-update-slice_fusion.shards, f32[8,128]{1,0:T(8,128)} %fusion.10.vec, bf16[256,1024]{1,0:T(8,128)(2,1)} %bitcast.65, ...), custom_call_target="tpu_custom_call" | custom-call | tf_op jit(solution)/shard_map/layer_kernel/pallas_call | solution.py:729
  253.7 0.0 copy-start.1
  253.7 0.0 copy-start.4
  253.8 0.0 copy-start.8
  253.8 0.0 copy-start.9
  253.8 1.4 slice_bitcast_fusion.12
  255.1 2.3 slice_bitcast_fusion.3
  257.5 1.1 pad_maximum_fusion
  258.5 0.0 copy-done.1
  258.5 0.0 copy-done.4
  258.6 0.0 copy-done.8
  258.6 0.0 copy-done.9
  258.6 0.0 copy-start.2
  258.6 0.0 copy-start.3
  258.6 2.9 %convert_select_fusion = bf16[2,1024,1024]{2,1,0:T(8,128)(2,1)} fusion(bf16[2,1024,1024]{2,1,0:T(8,128)(2,1)S(1)} %copy-done.1, pred[2,1024]{1,0:T(4,128)(4,1)S(1)} %copy-done.9, bf16[2,128,1024]{2,1,0:T(8,128)(2,1)S(1)} %bitcast.68, s32[2,128]{1,0:T(2,128)S(1)} %copy-done.8), kind=kOutput, calls=%fused_computation | convolution fusion | flops 541327360 | bytes 8915968 | tf_op jit(solution)/shard_map/scl,scd->sld/dot_general | solution.py:799
  261.5 0.5 copy-done.2
  262.0 0.4 copy-done.3
  262.4 2.8 %convert_select_fusion.1 = bf16[2,1024,1024]{2,1,0:T(8,128)(2,1)} fusion(bf16[2,1024,1024]{2,1,0:T(8,128)(2,1)S(1)} %copy-done.2, pred[2,1024]{1,0:T(4,128)(4,1)S(1)} %copy-done.9, bf16[2,128,1024]{2,1,0:T(8,128)(2,1)S(1)} %bitcast.67, s32[2,128]{1,0:T(2,128)S(1)} %copy-done.8), kind=kOutput, calls=%fused_computation.1 | convolution fusion | flops 541327360 | bytes 8915968 | tf_op jit(solution)/shard_map/scl,scd->sld/dot_general | solution.py:799
Async XLA Ops:
  0.6 8.6 %copy-start = (bf16[2,1024,1024]{2,1,0:T(8,128)(2,1)S(1)}, bf16[2,1024,1024]{2,1,0:T(8,128)(2,1)}, u32[]{:S(2)}) copy-start(bf16[2,1024,1024]{2,1,0:T(8,128)(2,1)} %param.25) | copy-start | bytes 12582916
  2.5 8.4 %copy-start.7 = (s32[2,128]{1,0:T(2,128)}, s32[2,128]{1,0:T(2,128)S(1)}, u32[]{:S(2)}) copy-start(s32[2,128]{1,0:T(2,128)S(1)} %get-tuple-element.20) | copy-start | bytes 3076
  5.4 5.5 %copy-start.10 = (bf16[128,256]{1,0:T(8,128)(2,1)S(1)}, bf16[128,256]{1,0:T(8,128)(2,1)}, u32[]{:S(2)}) copy-start(bf16[128,256]{1,0:T(8,128)(2,1)} %param.19) | copy-start | bytes 196612
  5.4 6.1 %copy-start.11 = (bf16[128,256]{1,0:T(8,128)(2,1)S(1)}, bf16[128,256]{1,0:T(8,128)(2,1)}, u32[]{:S(2)}) copy-start(bf16[128,256]{1,0:T(8,128)(2,1)} %param.20) | copy-start | bytes 196612
  5.4 6.7 %copy-start.12 = (bf16[128,256]{1,0:T(8,128)(2,1)S(1)}, bf16[128,256]{1,0:T(8,128)(2,1)}, u32[]{:S(2)}) copy-start(bf16[128,256]{1,0:T(8,128)(2,1)} %param.21) | copy-start | bytes 196612
  5.4 7.4 %copy-start.13 = (bf16[128,256]{1,0:T(8,128)(2,1)S(1)}, bf16[128,256]{1,0:T(8,128)(2,1)}, u32[]{:S(2)}) copy-start(bf16[128,256]{1,0:T(8,128)(2,1)} %param.22) | copy-start | bytes 196612
  9.3 4.2 %copy-start.5 = (bf16[128,1024]{1,0:T(8,128)(2,1)S(1)}, bf16[128,1024]{1,0:T(8,128)(2,1)}, u32[]{:S(2)}) copy-start(bf16[128,1024]{1,0:T(8,128)(2,1)} %param.23) | copy-start | bytes 786436
  9.3 4.8 %copy-start.6 = (bf16[128,1024]{1,0:T(8,128)(2,1)S(1)}, bf16[128,1024]{1,0:T(8,128)(2,1)}, u32[]{:S(2)}) copy-start(bf16[128,1024]{1,0:T(8,128)(2,1)} %param.24) | copy-start | bytes 786436
  253.7 4.8 %copy-start.1 = (bf16[2,1024,1024]{2,1,0:T(8,128)(2,1)S(1)}, bf16[2,1024,1024]{2,1,0:T(8,128)(2,1)}, u32[]{:S(2)}) copy-start(bf16[2,1024,1024]{2,1,0:T(8,128)(2,1)} %param.25) | copy-start | bytes 12582916
  253.7 4.8 %copy-start.4 = (bf16[256,1024]{1,0:T(8,128)(2,1)S(1)}, bf16[256,1024]{1,0:T(8,128)(2,1)}, u32[]{:S(2)}) copy-start(bf16[256,1024]{1,0:T(8,128)(2,1)} %get-tuple-element.16) | copy-start | bytes 1572868
  253.8 4.8 %copy-start.8 = (s32[2,128]{1,0:T(2,128)S(1)}, s32[2,128]{1,0:T(2,128)}, u32[]{:S(2)}) copy-start(s32[2,128]{1,0:T(2,128)} %copy-done.7) | copy-start | bytes 3076
  253.8 4.8 %copy-start.9 = (pred[2,1024]{1,0:T(4,128)(4,1)S(1)}, pred[2,1024]{1,0:T(4,128)(4,1)}, u32[]{:S(2)}) copy-start(pred[2,1024]{1,0:T(4,128)(4,1)} %broadcast_compare_fusion) | copy-start | bytes 6148
  258.6 3.4 %copy-start.2 = (bf16[2,1024,1024]{2,1,0:T(8,128)(2,1)S(1)}, bf16[2,1024,1024]{2,1,0:T(8,128)(2,1)}, u32[]{:S(2)}) copy-start(bf16[2,1024,1024]{2,1,0:T(8,128)(2,1)} %param.13) | copy-start | bytes 12582916
  258.6 3.8 %copy-start.3 = (bf16[256,1024]{1,0:T(8,128)(2,1)S(1)}, bf16[256,1024]{1,0:T(8,128)(2,1)}, u32[]{:S(2)}) copy-start(bf16[256,1024]{1,0:T(8,128)(2,1)} %get-tuple-element.15) | copy-start | bytes 1572868

commit v3 on v2

--- a/solution.py
+++ b/solution.py
@@ -83,15 +83,23 @@
     bits,
     ranks,
     chunks,
-    shards,
+    parts,
+    *refs,
+):
+    shards = refs[:6]
+    (
     vec,
-    picked,
-    grad_rows,
-    allowed,
+    routes,
+    pic_start,
+    activations,
+    cotangent,
     sums,
     vec_sum,
     new_rows,
     new_grads,
+    picked,
+    grad_rows,
+    allowed,
     held,
     from_core,
     from_z,
@@ -131,11 +139,13 @@
     in_z,
     out_v,
     in_v,
+    fetched,
     *from_path,
-):
+    ) = refs[6:]
     me, rank = lax.axis_index("dp"), lax.axis_index("tensor")
-    _, rows, width = shards.shape
+    rows, width = shards[0].shape
     count, full = picked.shape
+    length = activations.shape[1]
     seqs, caps, _ = allowed.shape
     half = full // 2
     seat, pair = bit_of(me, 0), lax.div(me, 2)
@@ -158,10 +168,13 @@
     mine = span(me, rows)
     columns = span(rank, width)
 
-    def keep_own(chunk):
-        return pltpu.make_async_copy(
-            shards.at[chunk], held.at[chunk, mine, columns], local.at[chunk]
-        )
+    def shard(chunk):
+        if chunk < 4:
+            return shards[chunk]
+        return shards[4 + chunk % 2].at[:, pl.ds((chunk - 4) // 2 * width, width)]
+
+    def keep_own(chunk, source=shards[0]):
+        return pltpu.make_async_copy(source, held.at[chunk, mine, columns], local.at[chunk])
 
     def bulk(chunk, depth, breadth):
         return held.at[chunk, pl.ds(0, depth), pl.ds(0, breadth)]
@@ -447,6 +460,49 @@
         for start in range(0, full, 128):
             part = source[:, start : start + 128].astype(F32)
             target[start : start + 128, :] = part.T.astype(BF16)
+
+    slab = pairs * rows
+    halves = length // slab
+
+    def fetch(source, seq, step, place):
+        def copy(index):
+            pltpu.make_async_copy(
+                source.at[seq, pl.ds(pl.multiple_of(index * rows, rows) + step * slab, rows)],
+                from_core.at[place, index],
+                fetched.at[place],
+            ).start()
+
+        each(pairs, copy)
+
+    def down_and_across(seq):
+        across = routes[pl.ds(rank * seqs + seq, 1), :].astype(F32)
+        return jnp.broadcast_to(across, (caps, caps)).T, across
+
+    def mask(seq):
+        down, across = down_and_across(seq)
+        begin = pic_start[rank * seqs + seq].astype(F32)
+        inside_down = (down >= begin) & (down < begin + PIC)
+        inside_across = (across >= begin) & (across < begin + PIC)
+        seen = (across <= down) | (inside_down & inside_across)
+        allowed[seq] = seen.astype(F32)
+
+    def pick(target, seq, place):
+        down, _ = down_and_across(seq)
+        column = lax.broadcasted_iota(jnp.int32, (caps, slab), 1).astype(F32)
+        for step in range(halves):
+            pltpu.make_async_copy(
+                from_core.at[place + step], from_core.at[place + step], fetched.at[place + step]
+            ).wait()
+
+        def body(part):
+            total = 0.0
+            for step in range(halves):
+                chosen = (down[:, 0:1] == column + step * slab).astype(F32).astype(BF16)
+                source = from_core[place + step, :, :, part].reshape(slab, block)
+                total = total + contract(chosen, source, 1, 0)
+            target[pl.ds(seq * caps, caps), part] = total.astype(BF16)
+
+        by_blocks(body)
 
     def prepare():
         def body(part):
@@ -651,10 +707,10 @@
             repeat(1 << bits, place)
 
     def start(chunk):
-        keep_own(chunk).start()
+        keep_own(chunk, shard(chunk)).start()
         for hop in range(1, ranks):
             remote(
-                shards.at[chunk],
+                shard(chunk),
                 held.at[chunk, mine, columns],
                 send_z.at[chunk],
                 recv_z.at[chunk],
@@ -663,9 +719,18 @@
 
     keep_vec = pltpu.make_async_copy(vec, vecs.at[me], local.at[chunks])
     keep_vec.start()
-    repeat(chunks, start)
+    for chunk in range(chunks):
+        start(chunk)
+    for which, source in enumerate((activations, cotangent)):
+        for seq in range(seqs):
+            for step in range(halves):
+                fetch(source, seq, step, (which * seqs + seq) * halves + step)
     keep_vec.wait()
     vec_gather()
+    for seq in range(seqs):
+        mask(seq)
+        for which, target in enumerate((picked, grad_rows)):
+            pick(target, seq, (which * seqs + seq) * halves)
     prepare()
     lead = AHEAD * bits
     first = lead + 5
@@ -718,25 +783,32 @@
     repeat(chunks, drain)
 
 
-def run_layer(bits, ranks, shards, vec, picked, grad_rows, allowed):
-    chunks, rows, width = shards.shape
+def run_layer(bits, ranks, shards, vec, routes, pic_start, activations, cotangent):
+    rows, width = shards[0].shape
+    parts = shards[4].shape[1] // width
+    chunks = 4 + 2 * parts
     depth, breadth, pairs = rows << bits, width * ranks, 1 << (bits - 1)
-    count, full = picked.shape
+    seqs, _, full = activations.shape
+    caps = routes.shape[1]
+    count = seqs * caps
     dma = pltpu.SemaphoreType.DMA
     low = pltpu.VMEM((count, full), BF16)
     turned = pltpu.VMEM((full, count), BF16)
     high = pltpu.VMEM((count, full), F32)
     return pl.pallas_call(
-        functools.partial(layer_kernel, bits, ranks, chunks),
+        functools.partial(layer_kernel, bits, ranks, chunks, parts),
         out_shape=[
             jax.ShapeDtypeStruct((chunks, rows, width), F32),
             jax.ShapeDtypeStruct((8, 128), F32),
             jax.ShapeDtypeStruct((count, full), BF16),
             jax.ShapeDtypeStruct((count, full), BF16),
         ],
-        in_specs=[ANY] + [VMEM] * 4,
+        in_specs=[ANY] * 6 + [VMEM] * 2 + [pl.BlockSpec(memory_space=pltpu.SMEM)] + [ANY] * 2,
         out_specs=[VMEM] * 4,
         scratch_shapes=[
+            low,
+            low,
+            pltpu.VMEM((seqs, caps, caps), F32),
             pltpu.VMEM((chunks, depth, breadth), BF16),
             pltpu.VMEM((RING, pairs, rows, breadth), BF16),
             pltpu.VMEM((chunks, ranks - 1, rows, width), BF16),
@@ -776,6 +848,7 @@
             dma((chunks,)),
             dma((bits + 1,)),
             dma((bits + 1,)),
+            dma((RING,)),
             *[
                 pltpu.VMEM((chunks, 2, pairs >> (stage + 1), rows, breadth // 2), BF16)
                 for stage in range(bits - 1)
@@ -785,18 +858,41 @@
             collective_id=1, has_side_effects=True, vmem_limit_bytes=67043328
         ),
         name="layer_kernel",
-    )(shards, vec, picked, grad_rows, allowed)
-
-
-def span_mask(positions, starts):
-    later = positions[:, None, :] <= positions[:, :, None]
-    begin = starts[:, None]
-    inside = (positions >= begin) & (positions < begin + PIC)
-    return later | inside[:, :, None] & inside[:, None, :]
-
-
-def dot(form, left, right):
-    return jnp.einsum(form, left, right, preferred_element_type=F32)
+    )(*shards, vec, routes, pic_start, activations, cotangent)
+
+
+def put_kernel(seqs, steps, routes, new_rows, new_grads, activations, cotangent, result, grad_input):
+    index = pl.program_id(0)
+    seq, step = lax.div(index, steps), lax.rem(index, steps)
+    size, caps = activations.shape[1], routes.shape[1]
+    place = routes[pl.ds(lax.axis_index("tensor") * seqs + seq, 1), :]
+    line = lax.broadcasted_iota(jnp.int32, (size, caps), 0) + step * size
+    chosen = (line == place).astype(F32)
+    routed = jnp.max(chosen, axis=-1, keepdims=True) > 0
+    chosen = chosen.astype(BF16)
+    for new, base, out in (
+        (new_rows, activations, result),
+        (new_grads, cotangent, grad_input),
+    ):
+        placed = contract(chosen, new[...], 1, 0)
+        out[0] = jnp.where(routed, placed, base[0].astype(F32)).astype(BF16)
+
+
+def put_rows(routes, new_rows, new_grads, activations, cotangent):
+    seqs, length, full = activations.shape
+    caps = routes.shape[1]
+    steps = 4
+    size = length // steps
+    large = pl.BlockSpec((1, size, full), lambda index: (index // steps, index % steps, 0))
+    small = pl.BlockSpec((caps, full), lambda index: (index // steps, 0))
+    return pl.pallas_call(
+        functools.partial(put_kernel, seqs, steps),
+        grid=(seqs * steps,),
+        out_shape=[jax.ShapeDtypeStruct(activations.shape, BF16)] * 2,
+        in_specs=[pl.BlockSpec(routes.shape, lambda index: (0, 0)), small, small, large, large],
+        out_specs=[large, large],
+        name="put_rows",
+    )(routes, new_rows, new_grads, activations, cotangent)
 
 
 def shards(
@@ -814,46 +910,24 @@
     w_down,
     cotangent,
 ):
-    seqs, length, features = activations.shape
     ranks = lax.axis_size("tensor")
     bits = lax.axis_size("dp").bit_length() - 1
-    rank = lax.axis_index("tensor")
     rows, width = w_query.shape
     parts = w_up.shape[1] // width
-    own_routes = lax.dynamic_slice_in_dim(routes, rank * seqs, seqs, 0)
-    own_start = lax.dynamic_slice_in_dim(pic_start, rank * seqs, seqs, 0)
-    caps = routes.shape[1]
-
     vec = jnp.stack([router_w, gain_attn, gain_mlp]).astype(F32)
     vec = jnp.pad(vec, ((0, 5), (0, 128 - rows)))
-    pieces = [w_query, w_key, w_value, w_proj]
-    for part in range(parts):
-        columns = slice(part * width, (part + 1) * width)
-        pieces += [w_up[:, columns], w_down[:, columns]]
-    chosen = (own_routes[:, :, None] == jnp.arange(length)[None, None, :]).astype(BF16)
-    picked = dot("scl,sld->scd", chosen, activations).astype(BF16)
-    grad_rows = dot("scl,sld->scd", chosen, cotangent).astype(BF16)
+    weights = (w_query, w_key, w_value, w_proj, w_up, w_down)
     sums, small, new_rows, new_grads = run_layer(
-        bits,
-        ranks,
-        jnp.stack(pieces),
-        vec,
-        picked.reshape(seqs * caps, features),
-        grad_rows.reshape(seqs * caps, features),
-        span_mask(own_routes, own_start).astype(F32),
+        bits, ranks, weights, vec, routes, pic_start, activations, cotangent
     )
-
-    def put(base, new):
-        placed = dot("scl,scd->sld", chosen, new.reshape(seqs, caps, features)).astype(BF16)
-        routed = jnp.sum(chosen.astype(F32), axis=1) > 0
-        return jnp.where(routed[:, :, None], placed, base)
+    result, grad_input = put_rows(routes, new_rows, new_grads, activations, cotangent)
 
     def side_by_side(first):
         return jnp.concatenate([sums[first + 2 * part] for part in range(parts)], axis=1)
 
     return (
-        put(activations, new_rows),
-        put(cotangent, new_grads),
+        result,
+        grad_input,
         small[3, :rows],
         small[4, :rows],
         small[5, :rows],

time: 265 us -> 255 us (0.962)
  Pallas kernels: 235 us -> 248 us
  matrix products: 11.1 us -> 0 us
  local copies, waits for them, and re-layouts: 12.3 us -> 3.6 us
  other arithmetic: 5.86 us -> 2.38 us
    pallas_call x1 -> x2, Pallas kernels: 235 us -> 248 us  [the longest x1 238 us: run_layer(): pl.pallas_call(functools.partial(layer_kernel, bits, ranks, chunks, parts...]
    dot_general x4 -> x0, matrix products: 11.1 us -> none  [dot(): return jnp.einsum(form, left, right, preferred_element_type=F32)]
    unnamed x39 -> x0, local copies, waits for them, and re-layouts: 7.98 us -> none
where the time goes in v3:
time: 255 us; the launch traced here: 254 us
  Pallas kernels  248 us (97%)
  local copies, waits for them, and re-layouts  3.6 us (1%)
    pallas_call x1, Pallas kernels, run_layer(): pl.pallas_call(functools.partial(layer_kernel, bits, ranks, chunks, parts...  238 us
    pallas_call x1, Pallas kernels, put_rows(): pl.pallas_call(functools.partial(put_kernel, seqs, steps), grid=(seqs * s...  10 us

profile of v3, /device:TPU:0, one launch (start us, length us, event | category | flops | bytes accessed | tf_op | source)
XLA Modules:
  0.0 254.5 jit_solution(2300250770202690465)
XLA Ops:
  0.6 1.3 fusion.5.refs_6_
  1.9 237.8 %layer_kernel.1 = (f32[12,128,256]{2,1,0:T(8,128)}, f32[8,128]{1,0:T(8,128)}, bf16[256,1024]{1,0:T(8,128)(2,1)}, bf16[256,1024]{1,0:T(8,128)(2,1)}) custom-call(bf16[128,256]{1,0:T(8,128)(2,1)} %refs_0_.1, bf16[128,256]{1,0:T(8,128)(2,1)} %refs_1_.1, bf16[128,256]{1,0:T(8,128)(2,1)} %refs_2_.1, bf16[128,256]{1,0:T(8,128)(2,1)} %refs_3_.1, ...), custom_call_target="tpu_custom_call" | custom-call | tf_op jit(solution)/shard_map/layer_kernel/pallas_call | solution.py:798
  239.7 1.3 slice_bitcast_fusion.12
  241.1 2.3 slice_bitcast_fusion.3
  243.4 1.1 pad_maximum_fusion
  244.4 10.0 %put_rows.1 = (bf16[2,1024,1024]{2,1,0:T(8,128)(2,1)}, bf16[2,1024,1024]{2,1,0:T(8,128)(2,1)}) custom-call(s32[8,128]{1,0:T(8,128)} %routes.1, bf16[256,1024]{1,0:T(8,128)(2,1)} %get-tuple-element.17.new_rows, bf16[256,1024]{1,0:T(8,128)(2,1)} %get-tuple-element.18.new_grads, bf16[2,1024,1024]{2,1,0:T(8,128)(2,1)} %activations.1, ...), custom_call_target="tpu_custom_call" | custom-call | tf_op jit(solution)/shard_map/put_rows/pallas_call | solution.py:888

commit v4 on v3

--- a/solution.py
+++ b/solution.py
@@ -12,7 +12,7 @@
 PIC = 256
 AHEAD = 2
 RING = 8
-PAUSE = 2
+PAUSE = 1
 MESH = pl.DeviceIdType.MESH
 ANY = pl.BlockSpec(memory_space=pl.ANY)
 VMEM = pl.BlockSpec(memory_space=pltpu.VMEM)
@@ -61,6 +61,10 @@
 
 def span(index, size):
     return pl.ds(pl.multiple_of(index * size, size), size)
+
+
+def sides(bits):
+    return (tuple(range(bits - 1, 1, -1)),) * 2
 
 
 def orders(bits):
@@ -109,7 +113,6 @@
     vec_z,
     params,
     gates,
-    scores_of,
     norm_one,
     qkv,
     context,
@@ -122,6 +125,25 @@
     grad_pre,
     mlp,
     grad_two,
+    slopes,
+    mlp_low,
+    grad_low,
+    mlp_in,
+    grad_in,
+    grad_attended,
+    grad_attended_t,
+    grad_context,
+    grad_qkv,
+    grad_one,
+    norm_one_t,
+    side_out,
+    side_in,
+    send_x,
+    recv_x,
+    act_out,
+    act_in,
+    out_x,
+    in_x,
     send_z,
     recv_z,
     send_p,
@@ -150,8 +172,11 @@
     half = full // 2
     seat, pair = bit_of(me, 0), lax.div(me, 2)
     pairs = 1 << (bits - 1)
-    paths = orders(bits)
-    back_paths = tuple(tuple(bit - 1 for bit in order[::-1]) for order in paths)
+    paths = (orders(bits), sides(bits))
+    back_paths = tuple(
+        tuple(tuple(bit - 1 for bit in order[::-1]) for order in kind) for kind in paths
+    )
+    side, beside = bit_of(me, 1), flipped(me, 1)
     tile = 32
     block = 256
     blocks = full // block
@@ -168,10 +193,11 @@
     mine = span(me, rows)
     columns = span(rank, width)
 
-    def shard(chunk):
+    def shard(chunk, which):
         if chunk < 4:
             return shards[chunk]
-        return shards[4 + chunk % 2].at[:, pl.ds((chunk - 4) // 2 * width, width)]
+        index = which * (parts // 2) + (chunk - 4) // 2
+        return shards[4 + chunk % 2].at[:, span(index, width)]
 
     def keep_own(chunk, source=shards[0]):
         return pltpu.make_async_copy(source, held.at[chunk, mine, columns], local.at[chunk])
@@ -179,16 +205,48 @@
     def bulk(chunk, depth, breadth):
         return held.at[chunk, pl.ds(0, depth), pl.ds(0, breadth)]
 
-    def z_copy(chunk):
-        part = bulk(chunk, rows, width * (ranks - 1))
+    def send_z_of(chunk, source, index):
+        for hop in range(1, ranks):
+            remote(
+                source,
+                held.at[chunk, span(index, rows), columns],
+                send_z.at[chunk],
+                recv_z.at[chunk],
+                (me, lax.rem(rank + hop, ranks)),
+            ).start()
+
+    def x_copy(chunk):
+        part = bulk(chunk, rows, width)
+        return remote(part, part, send_x.at[chunk], recv_x.at[chunk], (me, rank))
+
+    def start(chunk):
+        keep_own(chunk, shard(chunk, side)).start()
+        if chunk >= 4:
+            remote(
+                shard(chunk, 1 - side),
+                held.at[chunk, mine, columns],
+                send_x.at[chunk],
+                recv_x.at[chunk],
+                (beside, rank),
+            ).start()
+
+    def start_z(chunk):
+        if chunk >= 4:
+            x_copy(chunk).wait_recv()
+            send_z_of(chunk, held.at[chunk, span(beside, rows), columns], beside)
+        send_z_of(chunk, shard(chunk, side), me)
+
+    def z_copy(chunk, kind):
+        part = bulk(chunk, rows << kind, width * (ranks - 1))
         return remote(part, part, send_z.at[chunk], recv_z.at[chunk], (me, rank))
 
-    def send_path(chunk, colour, stage):
-        order = paths[colour]
+    def send_path(chunk, kind, colour, stage):
+        order = paths[kind][colour]
+        earlier = order[:stage] + (1,) * kind
         other = (flipped(me, order[stage]), rank)
 
         def send(step):
-            index = cleared(me, order[:stage]) + spread(step, order[:stage])
+            index = cleared(me, earlier) + spread(step, earlier)
             part = held.at[chunk, span(index, rows), pl.ds(colour * half, half)]
             remote(
                 part,
@@ -198,10 +256,10 @@
                 other,
             ).start()
 
-        each(1 << stage, send)
-
-    def path_copy(chunk, colour, stage):
-        part = bulk(chunk, rows << stage, half)
+        each(1 << len(earlier), send)
+
+    def path_copy(chunk, kind, colour, stage):
+        part = bulk(chunk, rows << (stage + kind), half)
         return remote(
             part,
             part,
@@ -223,32 +281,39 @@
         part = bulk(chunk, rows << (bits - 1), full)
         return remote(part, part, send_c.at[chunk], recv_c.at[chunk], (me, rank))
 
-    def all_sent(chunk):
+    def all_sent(chunk, kind):
+        z_copy(chunk, kind).wait_send()
+        if kind:
+            x_copy(chunk).wait_send()
         for colour in range(2):
-            for stage in range(bits - 1):
-                path_copy(chunk, colour, stage).wait_send()
+            for stage in range(bits - 1 - kind):
+                path_copy(chunk, kind, colour, stage).wait_send()
         core_copy(chunk).wait_send()
 
-    def gather_stage(chunk, stage):
-        if stage == 0:
+    def gather_stage(chunk, kind, stage):
+        if stage < kind:
+            return
+        if stage == kind:
             keep_own(chunk).wait()
-            z_copy(chunk).wait_recv()
+            z_copy(chunk, kind).wait_recv()
         elif stage < bits:
             for colour in range(2):
-                path_copy(chunk, colour, stage - 1).wait_recv()
+                path_copy(chunk, kind, colour, stage - 1 - kind).wait_recv()
         else:
             core_copy(chunk).wait_recv()
         if stage < bits - 1:
             for colour in range(2):
-                send_path(chunk, colour, stage)
+                send_path(chunk, kind, colour, stage - kind)
         elif stage == bits - 1:
             send_core(chunk)
 
+    units = chunks - 4
+
     def turn(item):
-        return jnp.where(item < chunks - 4, item, item - PAUSE)
+        return jnp.where(item < units, item, item - PAUSE)
 
     def slot(item):
-        return jnp.where(item < chunks - 4, item + 4, item - PAUSE - chunks + 4)
+        return jnp.where(item < units, item + 4, lax.rem(item - PAUSE - units + 3, 4))
 
     def give_core(item):
         def send(step):
@@ -283,17 +348,17 @@
             ),
         )
 
-    def members(stage, order, step, kept):
-        bit, later = order[stage], order[stage + 1 :]
-        index = pair if kept else flipped(pair, bit)
+    def members(kind, colour, stage, step, kept):
+        order = back_paths[kind][colour]
+        later = order[stage + 1 :] + (0,) * kind
+        index = pair if kept else flipped(pair, order[stage])
         return cleared(index, later) + spread(step, later)
 
-    def give_path(item, colour, stage):
-        order = back_paths[colour]
-        other = (2 * flipped(pair, order[stage]) + seat, rank)
+    def give_path(item, kind, colour, stage):
+        other = (2 * flipped(pair, back_paths[kind][colour][stage]) + seat, rank)
 
         def send(step):
-            index = members(stage, order, step, False)
+            index = members(kind, colour, stage, step, False)
             remote(
                 held.at[
                     slot(item), span(2 * index + seat, rows), pl.ds(colour * half, half)
@@ -304,7 +369,7 @@
                 other,
             ).start()
 
-        each(1 << (len(order) - stage - 1), send)
+        each(pairs >> (stage + 1), send)
 
     def given_path(item, colour, stage):
         part = from_path[stage].at[turn(item), colour]
@@ -316,72 +381,95 @@
             (me, rank),
         )
 
-    def add_path(item, colour, stage):
-        order = back_paths[colour]
+    def add_path(item, kind, colour, stage):
         repeat(
-            1 << (len(order) - stage - 1),
+            pairs >> (stage + 1),
             lambda step: add_to(
                 item,
-                members(stage, order, step, True),
+                members(kind, colour, stage, step, True),
                 pl.ds(colour * half, half),
                 from_path[stage].at[turn(item), colour, step],
             ),
         )
 
-    def give_across(item):
+    def give_across(item, kind):
         for hop in range(1, ranks):
             to = lax.rem(rank + hop, ranks)
-            remote(
-                held.at[slot(item), mine, span(to, width)],
-                from_z.at[turn(item), hop - 1],
-                out_z.at[turn(item)],
-                in_z.at[turn(item)],
-                (me, to),
-            ).start()
-
-    def given_across(item):
-        part = from_z.at[turn(item)]
+            for which in range(1 + kind):
+                remote(
+                    held.at[slot(item), span((me, beside)[which], rows), span(to, width)],
+                    from_z.at[turn(item), (hop - 1) * (1 + kind) + which],
+                    out_z.at[turn(item)],
+                    in_z.at[turn(item)],
+                    (me, to),
+                ).start()
+
+    def given_across(item, kind):
+        part = from_z.at[turn(item), pl.ds(0, (ranks - 1) * (1 + kind))]
         return remote(part, part, out_z.at[turn(item)], in_z.at[turn(item)], (me, rank))
 
-    def finish(item):
-        total = held[slot(item), mine, columns].astype(F32)
+    def total_of(item, kind, which):
+        total = held[slot(item), span((me, beside)[which], rows), columns].astype(F32)
         for hop in range(1, ranks):
-            total = total + from_z[turn(item), hop - 1].astype(F32)
-        sums[slot(item)] = total
-
-    def scatter_stage(item, stage):
+            total = total + from_z[turn(item), (hop - 1) * (1 + kind) + which].astype(F32)
+        return total
+
+    def unit_place(item, which):
+        return 4 + 2 * (which * (parts // 2) + lax.div(item, 2)) + lax.rem(item, 2)
+
+    def side_copy(item):
+        return remote(
+            side_out.at[item], side_in.at[item], out_x.at[item], in_x.at[item], (beside, rank)
+        )
+
+    def scatter_stage(item, kind, stage):
         if stage == 1:
             given_core(item).wait_recv()
             add_core(item)
-        elif 1 < stage <= bits:
+        elif 1 < stage <= bits - kind:
             for colour in range(2):
                 given_path(item, colour, stage - 2).wait_recv()
-                add_path(item, colour, stage - 2)
-        elif stage == bits + 1:
-            given_across(item).wait_recv()
-            finish(item)
+                add_path(item, kind, colour, stage - 2)
+        elif stage == bits - kind + 1:
+            given_across(item, kind).wait_recv()
+            if kind:
+                side_out[item] = total_of(item, kind, 1).astype(BF16)
+                side_copy(item).start()
+                sums[unit_place(item, side)] = total_of(item, kind, 0)
+            else:
+                sums[slot(item)] = total_of(item, kind, 0)
+        elif stage == bits - kind + 2:
+            side_copy(item).wait_recv()
+            sums[unit_place(item, 1 - side)] = side_in[item].astype(F32)
         if stage == 0:
             give_core(item)
-        elif stage < bits:
+        elif stage < bits - kind:
             for colour in range(2):
-                give_path(item, colour, stage - 1)
-        elif stage == bits:
-            give_across(item)
-
-    def vec_gather():
-        path = tuple(range(bits - 1, -1, -1))
-        for stage, bit in enumerate(path):
-            other = (flipped(me, bit), rank)
-
-            def send(step, stage=stage, other=other):
-                index = cleared(me, path[:stage]) + spread(step, path[:stage])
+                give_path(item, kind, colour, stage - 1)
+        elif stage == bits - kind:
+            give_across(item, kind)
+
+    vec_ways = tuple(range(bits - 1, -1, -1))
+
+    def vec_gather(stage):
+        if stage > 0:
+            part = vecs.at[pl.ds(0, 1 << (stage - 1))]
+            remote(part, part, send_v.at[stage - 1], recv_v.at[stage - 1], (me, rank)).wait()
+        if stage < bits:
+
+            def send(step):
+                index = cleared(me, vec_ways[:stage]) + spread(step, vec_ways[:stage])
                 remote(
-                    vecs.at[index], vecs.at[index], send_v.at[stage], recv_v.at[stage], other
+                    vecs.at[index],
+                    vecs.at[index],
+                    send_v.at[stage],
+                    recv_v.at[stage],
+                    (flipped(me, vec_ways[stage]), rank),
                 ).start()
 
             each(1 << stage, send)
-            part = vecs.at[pl.ds(0, 1 << stage)]
-            remote(part, part, send_v.at[stage], recv_v.at[stage], other).wait()
+
+    def spell_params():
         params[...] = jnp.zeros_like(params)
         lane = lax.broadcasted_iota(jnp.int32, (128, full), 0)
         column = lax.broadcasted_iota(jnp.int32, (128, full), 1)
@@ -390,7 +478,11 @@
             chosen = ((lane < rows) & (column == index * rows + lane)).astype(F32).astype(BF16)
             params[...] += contract(vecs[index].astype(BF16), chosen, 1, 0)
 
-        repeat(1 << bits, place)
+        if rows == 128:
+            for index in range(1 << bits):
+                params[:, index * rows : (index + 1) * rows] = vecs[index]
+        else:
+            repeat(1 << bits, place)
 
     vec_path_of = tuple(range(bits))
 
@@ -456,10 +548,30 @@
     def wide(values):
         return jnp.broadcast_to(values, (values.shape[0], 128))
 
-    def transpose_to(target, source):
-        for start in range(0, full, 128):
-            part = source[:, start : start + 128].astype(F32)
-            target[start : start + 128, :] = part.T.astype(BF16)
+    def transpose_to(target, source, first=0):
+        def turn_over(index):
+            part = span(index, 128)
+            values = source[first : first + count, part].astype(F32)
+            target[part, first : first + count] = values.T.astype(BF16)
+
+        repeat(full // 128, turn_over)
+
+    def to_beside(which, source, target):
+        return remote(source, target, act_out.at[which], act_in.at[which], (beside, rank))
+
+    own_rows, their_rows = pl.ds(0, count), pl.ds(count, count)
+
+    def branch_copy():
+        return to_beside(0, branch.at[own_rows], branch.at[their_rows])
+
+    def norm_copy():
+        return to_beside(1, norm_two.at[own_rows], norm_two.at[their_rows])
+
+    def grad_copy():
+        return to_beside(2, grad_low, grad_in)
+
+    def mlp_copy():
+        return to_beside(3, mlp_low, mlp_in)
 
     slab = pairs * rows
     halves = length // slab
@@ -514,6 +626,7 @@
             branch[part] = (gate * grad_rows[part].astype(F32)).astype(BF16)
 
         by_rows(body)
+        branch_copy().start()
         transpose_to(branch_t, branch)
 
     def project(which):
@@ -558,30 +671,62 @@
         def rest(part):
             values = picked[part].astype(F32) + attended[part]
             norm_two[part] = (values * inverse_of(values) * gain_two()).astype(BF16)
-            mlp[part] = jnp.zeros((tile, full), F32)
-            grad_two[part] = jnp.zeros((tile, full), F32)
 
         by_rows(rest)
+        norm_copy().start()
         transpose_to(norm_two_t, norm_two)
-
-    def feed_forward(up, down):
-        def units(part):
-            pre = contract(norm_two[...], held[up, :, part], 1, 0)
+        mlp[...] = jnp.zeros_like(mlp)
+        grad_two[...] = jnp.zeros_like(grad_two)
+
+    def by_lines(body):
+        repeat(2 * blocks, lambda i: body(span(lax.rem(i, 2), count), span(lax.div(i, 2), block)))
+
+    def go_up(up):
+        @pl.when(up == 4)
+        def _():
+            branch_copy().wait_recv()
+            transpose_to(branch_t, branch, count)
+            norm_copy().wait_recv()
+            transpose_to(norm_two_t, norm_two, count)
+
+        def units_of(lines, part):
+            pre = contract(norm_two[lines], held[up, :, part], 1, 0)
             bell = 0.5 * (1.0 + lax.erf(pre * inv_root_two))
-            slope = bell + pre * jnp.exp(-0.5 * pre * pre) * inv_root_two_pi
-            hidden[:, part] = (pre * bell).astype(BF16)
-            grad_hidden = contract(branch[...], held[down, :, part], 1, 0)
-            grad_pre[:, part] = (grad_hidden * slope).astype(BF16)
-
-        by_blocks(units)
-
-        def outputs(part):
-            mlp[:, part] += contract(hidden[...], held[down, part, :], 1, 1)
-            grad_two[:, part] += contract(grad_pre[...], held[up, part, :], 1, 1)
-
-        by_blocks(outputs)
-        all_sent(up)
-        all_sent(down)
+            slopes[lines, part] = bell + pre * jnp.exp(-0.5 * pre * pre) * inv_root_two_pi
+            hidden[lines, part] = (pre * bell).astype(BF16)
+
+        by_lines(units_of)
+
+    def go_down(up, down):
+        def units_of(lines, part):
+            grad_hidden = contract(branch[lines], held[down, :, part], 1, 0)
+            grad_pre[lines, part] = (grad_hidden * slopes[lines, part]).astype(BF16)
+
+        by_lines(units_of)
+
+        def add_out(target, source, weight, lines):
+            def body(part):
+                target[lines, part] += contract(source[lines], held[weight, part, :], 1, 1)
+
+            by_blocks(body)
+
+        def pass_on(source, target, copy):
+            @pl.when(down == chunks - 1)
+            def _():
+                def body(part):
+                    target[part] = source[pl.ds(part.start + count, tile)].astype(BF16)
+
+                by_rows(body)
+                copy().start()
+
+        add_out(grad_two, grad_pre, up, their_rows)
+        pass_on(grad_two, grad_low, grad_copy)
+        add_out(mlp, hidden, down, their_rows)
+        pass_on(mlp, mlp_low, mlp_copy)
+        add_out(grad_two, grad_pre, up, own_rows)
+        add_out(mlp, hidden, down, own_rows)
+        all_sent(up, 1)
+        all_sent(down, 1)
 
         def gradients(part):
             held[down, :, part] = contract(branch_t[...], hidden[:, part], 1, 0).astype(BF16)
@@ -592,27 +737,21 @@
     small = params
 
     def enter_back():
-        grad_attended, grad_attended_t, grad_context = norm_two, norm_two_t, hidden
         small[3:6, :] = jnp.zeros((3, full), F32)
+        grad_copy().wait_recv()
 
         def body(part):
             values = picked[part].astype(F32)
-            gate = gates[part, 0:1]
-            delta = attended[part] + mlp[part]
-            new_rows[part] = (values + gate * delta).astype(BF16)
-            rows_in = grad_rows[part].astype(F32)
-            score = jnp.sum(rows_in * delta, axis=-1, keepdims=True) * gate * (1.0 - gate)
-            scores_of[part] = wide(score)
-            small[3:4, :] += jnp.sum(score * values, axis=0, keepdims=True)
             residual = values + attended[part]
             inverse = inverse_of(residual)
-            grad = grad_two[part]
+            grad = grad_two[part] + grad_in[part].astype(F32)
             small[5:6, :] += jnp.sum(grad * residual * inverse, axis=0, keepdims=True)
             scaled = grad * gain_two()
             mean = jnp.mean(scaled * residual, axis=-1, keepdims=True)
             grad_mid = inverse * scaled - residual * (inverse * inverse * inverse * mean)
             grad_two[part] = grad_mid
-            grad_attended[part] = (gate * rows_in + grad_mid).astype(BF16)
+            rows_in = grad_rows[part].astype(F32)
+            grad_attended[part] = (gates[part, 0:1] * rows_in + grad_mid).astype(BF16)
 
         by_rows(body)
         transpose_to(grad_attended_t, grad_attended)
@@ -622,17 +761,15 @@
 
         by_blocks(through)
         for chunk in range(4):
-            all_sent(chunk)
+            all_sent(chunk, 0)
 
         def weights(part):
             held[3, :, part] = contract(grad_attended_t[...], context[:, part], 1, 0).astype(BF16)
 
         by_blocks(weights)
+        give_core(jnp.int32(units + PAUSE))
 
     def attend_back():
-        grad_context = hidden
-        grads = (branch, grad_pre, context)
-
         def body(index):
             part = span(index, 2 * HD)
             for seq in range(seqs):
@@ -650,20 +787,17 @@
                     grad_q = grad_q + contract(grad_scores, own_lanes(keys, head), 1, 0)
                     grad_k = grad_k + contract(grad_scores, own_lanes(queries, head), 0, 0)
                 scale = 1.0 / math.sqrt(HD)
-                grads[0][place, part] = (grad_q * scale).astype(BF16)
-                grads[1][place, part] = (grad_k * scale).astype(BF16)
-                grads[2][place, part] = grad_v.astype(BF16)
+                grad_qkv[0, place, part] = (grad_q * scale).astype(BF16)
+                grad_qkv[1, place, part] = (grad_k * scale).astype(BF16)
+                grad_qkv[2, place, part] = grad_v.astype(BF16)
 
         repeat(full // (2 * HD), body)
 
     def leave_back():
-        grads = (branch, grad_pre, context)
-        grad_one, norm_one_t = mlp, branch_t
-
         def through(part):
-            total = contract(grads[0][...], held[0, part, :], 1, 1)
+            total = contract(grad_qkv[0], held[0, part, :], 1, 1)
             for which in (1, 2):
-                total = total + contract(grads[which][...], held[which, part, :], 1, 1)
+                total = total + contract(grad_qkv[which], held[which, part, :], 1, 1)
             grad_one[:, part] = total
 
         by_blocks(through)
@@ -671,22 +805,32 @@
 
         def weights(part):
             for which in range(3):
-                held[which, :, part] = contract(norm_one_t[...], grads[which][:, part], 1, 0).astype(
+                held[which, :, part] = contract(norm_one_t[...], grad_qkv[which, :, part], 1, 0).astype(
                     BF16
                 )
 
         by_blocks(weights)
+        for item in range(units + PAUSE + 1, units + PAUSE + 4):
+            give_core(jnp.int32(item))
+
+    def close():
+        mlp_copy().wait_recv()
 
         def body(part):
             values = picked[part].astype(F32)
+            rows_in = grad_rows[part].astype(F32)
+            gate = gates[part, 0:1]
+            delta = attended[part] + (mlp[part] + mlp_in[part].astype(F32))
+            new_rows[part] = (values + gate * delta).astype(BF16)
+            score = jnp.sum(rows_in * delta, axis=-1, keepdims=True) * gate * (1.0 - gate)
+            small[3:4, :] += jnp.sum(score * values, axis=0, keepdims=True)
             inverse = inverse_of(values)
             grad = grad_one[part]
             small[4:5, :] += jnp.sum(grad * values * inverse, axis=0, keepdims=True)
             scaled = grad * gain_one()
             mean = jnp.mean(scaled * values, axis=-1, keepdims=True)
             grad_norm = inverse * scaled - values * (inverse * inverse * inverse * mean)
-            score = scores_of[part, 0:1]
-            total = grad_rows[part].astype(F32) + grad_two[part] + grad_norm + score * router()
+            total = rows_in + grad_two[part] + grad_norm + score * router()
             new_grads[part] = total.astype(BF16)
 
         by_rows(body)
@@ -706,36 +850,24 @@
 
             repeat(1 << bits, place)
 
-    def start(chunk):
-        keep_own(chunk, shard(chunk)).start()
-        for hop in range(1, ranks):
-            remote(
-                shard(chunk),
-                held.at[chunk, mine, columns],
-                send_z.at[chunk],
-                recv_z.at[chunk],
-                (me, lax.rem(rank + hop, ranks)),
-            ).start()
-
     keep_vec = pltpu.make_async_copy(vec, vecs.at[me], local.at[chunks])
     keep_vec.start()
-    for chunk in range(chunks):
+    for chunk in range(4):
+        start(chunk)
+        start_z(chunk)
+    for chunk in range(4, chunks):
         start(chunk)
     for which, source in enumerate((activations, cotangent)):
         for seq in range(seqs):
             for step in range(halves):
                 fetch(source, seq, step, (which * seqs + seq) * halves + step)
     keep_vec.wait()
-    vec_gather()
-    for seq in range(seqs):
-        mask(seq)
-        for which, target in enumerate((picked, grad_rows)):
-            pick(target, seq, (which * seqs + seq) * halves)
-    prepare()
+    vec_gather(0)
+
     lead = AHEAD * bits
     first = lead + 5
     items = chunks + PAUSE
-    vec_first = lead + chunks + PAUSE + 1
+    vec_first = lead + chunks + 6
 
     def tick(now, _):
         for stage in range(bits, -1, -1):
@@ -743,27 +875,48 @@
 
             @pl.when((chunk >= 0) & (chunk < chunks))
             def _(chunk=chunk, stage=stage):
-                gather_stage(chunk, stage)
+                pl.when(chunk < 4)(lambda: gather_stage(chunk, 0, stage))
+                pl.when(chunk >= 4)(lambda: gather_stage(chunk, 1, stage))
+
+        for stage in range(1, bits + 1):
+            pl.when(now == stage)(functools.partial(vec_gather, stage))
+
+        @pl.when(now == 1)
+        def _():
+            for chunk in range(4, chunks):
+                start_z(chunk)
+
+        for seq in range(seqs):
+            for which, target in enumerate((picked, grad_rows)):
+                order = 2 * seq + which
+                place = (which * seqs + seq) * halves
+                pl.when(now == order)(functools.partial(pick, target, seq, place))
+            pl.when(now == 2 * seq)(functools.partial(mask, seq))
+
+        @pl.when(now == max(bits, 2 * seqs - 1) + 1)
+        def _():
+            spell_params()
+            prepare()
 
         whole = now - lead
         pl.when((whole >= 0) & (whole < 3))(lambda: project(whole))
         pl.when(whole == 2)(attend)
         pl.when(whole == 3)(leave_attention)
-        pl.when((whole >= 5) & (whole < chunks) & (lax.rem(whole, 2) == 1))(
-            lambda: feed_forward(whole - 1, whole)
-        )
+        units_in = (whole >= 4) & (whole < chunks)
+        pl.when(units_in & (lax.rem(whole, 2) == 0))(lambda: go_up(whole))
+        pl.when(units_in & (lax.rem(whole, 2) == 1))(lambda: go_down(whole - 1, whole))
         for stage in range(bits + 1, -1, -1):
             item = now - first - AHEAD * stage
             inside = (item >= 0) & (item < items)
-            paused = (item >= chunks - 4) & (item < chunks - 4 + PAUSE)
-
-            @pl.when(inside & jnp.logical_not(paused))
-            def _(item=item, stage=stage):
-                scatter_stage(item, stage)
-
-        pl.when(whole == chunks)(enter_back)
-        pl.when(whole == chunks + 1)(attend_back)
-        pl.when(whole == chunks + 2)(leave_back)
+            pl.when(inside & (item < units))(functools.partial(scatter_stage, item, 1, stage))
+            if stage > 0:
+                late = inside & (item >= units + PAUSE)
+                pl.when(late)(functools.partial(scatter_stage, item, 0, stage))
+
+        pl.when(whole == chunks + 1)(enter_back)
+        pl.when(whole == chunks + 2)(attend_back)
+        pl.when(whole == chunks + 3)(leave_back)
+        pl.when(whole == chunks + 5)(close)
         for stage in range(bits + 1):
             pl.when(now == vec_first + AHEAD * stage)(functools.partial(vec_stage, stage))
         pl.when(now == vec_first + AHEAD * (bits + 1))(vec_finish)
@@ -771,22 +924,28 @@
     last = max(first + items - 1 + AHEAD * (bits + 1), vec_first + AHEAD * (bits + 1))
     lax.fori_loop(0, last + 1, tick, None)
 
-    def drain(chunk):
-        z_copy(chunk).wait_send()
-        item = jnp.where(chunk < chunks - 4, chunk, chunk + PAUSE)
+    branch_copy().wait_send()
+    norm_copy().wait_send()
+    grad_copy().wait_send()
+    mlp_copy().wait_send()
+
+    def drain(item, kind):
         given_core(item).wait_send()
         for colour in range(2):
-            for stage in range(bits - 1):
+            for stage in range(bits - 1 - kind):
                 given_path(item, colour, stage).wait_send()
-        given_across(item).wait_send()
-
-    repeat(chunks, drain)
+        given_across(item, kind).wait_send()
+        if kind:
+            side_copy(item).wait_send()
+
+    repeat(units, lambda item: drain(item, 1))
+    repeat(4, lambda item: drain(item + units + PAUSE, 0))
 
 
 def run_layer(bits, ranks, shards, vec, routes, pic_start, activations, cotangent):
     rows, width = shards[0].shape
     parts = shards[4].shape[1] // width
-    chunks = 4 + 2 * parts
+    chunks = 4 + parts
     depth, breadth, pairs = rows << bits, width * ranks, 1 << (bits - 1)
     seqs, _, full = activations.shape
     caps = routes.shape[1]
@@ -795,10 +954,13 @@
     low = pltpu.VMEM((count, full), BF16)
     turned = pltpu.VMEM((full, count), BF16)
     high = pltpu.VMEM((count, full), F32)
+    low_two = pltpu.VMEM((2 * count, full), BF16)
+    turned_two = pltpu.VMEM((full, 2 * count), BF16)
+    high_two = pltpu.VMEM((2 * count, full), F32)
     return pl.pallas_call(
         functools.partial(layer_kernel, bits, ranks, chunks, parts),
         out_shape=[
-            jax.ShapeDtypeStruct((chunks, rows, width), F32),
+            jax.ShapeDtypeStruct((4 + 2 * parts, rows, width), F32),
             jax.ShapeDtypeStruct((8, 128), F32),
             jax.ShapeDtypeStruct((count, full), BF16),
             jax.ShapeDtypeStruct((count, full), BF16),
@@ -811,26 +973,44 @@
             pltpu.VMEM((seqs, caps, caps), F32),
             pltpu.VMEM((chunks, depth, breadth), BF16),
             pltpu.VMEM((RING, pairs, rows, breadth), BF16),
-            pltpu.VMEM((chunks, ranks - 1, rows, width), BF16),
+            pltpu.VMEM((chunks, 2 * (ranks - 1), rows, width), BF16),
             pltpu.VMEM((1 << bits, 8, 128), F32),
             pltpu.VMEM((1 << bits, 8, 128), F32),
             pltpu.VMEM((1 << bits, 8, 128), F32),
             pltpu.VMEM((ranks - 1, 8, 128), F32),
             pltpu.VMEM((8, full), F32),
             pltpu.VMEM((count, 128), F32),
-            pltpu.VMEM((count, 128), F32),
             low,
             pltpu.VMEM((3, count, full), BF16),
             low,
             high,
+            low_two,
+            turned_two,
+            low_two,
+            turned_two,
+            low_two,
+            low_two,
+            high_two,
+            high_two,
+            high_two,
+            low,
+            low,
+            low,
+            low,
             low,
             turned,
             low,
+            pltpu.VMEM((3, count, full), BF16),
+            high,
             turned,
-            low,
-            low,
-            high,
-            high,
+            pltpu.VMEM((parts, rows, width), BF16),
+            pltpu.VMEM((parts, rows, width), BF16),
+            dma((chunks,)),
+            dma((chunks,)),
+            dma((4,)),
+            dma((4,)),
+            dma((parts,)),
+            dma((parts,)),
             dma((chunks,)),
             dma((chunks,)),
             dma((chunks, 2, bits - 1)),

time: 255 us -> 240 us (0.941)
  Pallas kernels: 248 us -> 233 us
    pallas_call x1, Pallas kernels: 238 us -> 223 us  [run_layer(): pl.pallas_call(functools.partial(layer_kernel, bits, ranks, chunks, parts...]
where the time goes in v4:
time: 240 us
  Pallas kernels  233 us (97%)
  local copies, waits for them, and re-layouts  3.6 us (2%)
    pallas_call x1, Pallas kernels, run_layer(): pl.pallas_call(functools.partial(layer_kernel, bits, ranks, chunks, parts...  223 us
    pallas_call x1, Pallas kernels, put_rows(): pl.pallas_call(functools.partial(put_kernel, seqs, steps), grid=(seqs * s...  10 us

profile of v4, /device:TPU:0, one launch (start us, length us, event | category | flops | bytes accessed | tf_op | source)
XLA Modules:
  0.0 240.0 jit_solution(1643396602201129193)
XLA Ops:
  0.6 1.3 fusion.5.refs_6_
  1.9 223.3 %layer_kernel.1 = (f32[12,128,256]{2,1,0:T(8,128)}, f32[8,128]{1,0:T(8,128)}, bf16[256,1024]{1,0:T(8,128)(2,1)}, bf16[256,1024]{1,0:T(8,128)(2,1)}) custom-call(bf16[128,256]{1,0:T(8,128)(2,1)} %refs_0_.1, bf16[128,256]{1,0:T(8,128)(2,1)} %refs_1_.1, bf16[128,256]{1,0:T(8,128)(2,1)} %refs_2_.1, bf16[128,256]{1,0:T(8,128)(2,1)} %refs_3_.1, ...), custom_call_target="tpu_custom_call" | custom-call | tf_op jit(solution)/shard_map/layer_kernel/pallas_call | solution.py:960
  225.3 1.3 slice_bitcast_fusion.12
  226.6 2.3 slice_bitcast_fusion.3
  228.9 1.1 pad_maximum_fusion
  230.0 10.0 %put_rows.1 = (bf16[2,1024,1024]{2,1,0:T(8,128)(2,1)}, bf16[2,1024,1024]{2,1,0:T(8,128)(2,1)}) custom-call(s32[8,128]{1,0:T(8,128)} %routes.1, bf16[256,1024]{1,0:T(8,128)(2,1)} %get-tuple-element.17.new_rows, bf16[256,1024]{1,0:T(8,128)(2,1)} %get-tuple-element.18.new_grads, bf16[2,1024,1024]{2,1,0:T(8,128)(2,1)} %activations.1, ...), custom_call_target="tpu_custom_call" | custom-call | tf_op jit(solution)/shard_map/put_rows/pallas_call | solution.py:1068

commit v5 on v4

--- a/solution.py
+++ b/solution.py
@@ -10,9 +10,7 @@
 
 HD = 64
 PIC = 256
-AHEAD = 2
 RING = 8
-PAUSE = 1
 MESH = pl.DeviceIdType.MESH
 ANY = pl.BlockSpec(memory_space=pl.ANY)
 VMEM = pl.BlockSpec(memory_space=pltpu.VMEM)
@@ -310,16 +308,16 @@
     units = chunks - 4
 
     def turn(item):
-        return jnp.where(item < units, item, item - PAUSE)
+        return item
 
     def slot(item):
-        return jnp.where(item < units, item + 4, lax.rem(item - PAUSE - units + 3, 4))
+        return item + 4 if item < units else (item - units + 3) % 4
 
     def give_core(item):
         def send(step):
             remote(
                 held.at[slot(item), span(2 * step + 1 - seat, rows)],
-                from_core.at[lax.rem(turn(item), RING), step],
+                from_core.at[turn(item) % RING, step],
                 out_c.at[turn(item)],
                 in_c.at[turn(item)],
                 (flipped(me, 0), rank),
@@ -328,7 +326,7 @@
         each(pairs, send)
 
     def given_core(item):
-        part = from_core.at[lax.rem(turn(item), RING)]
+        part = from_core.at[turn(item) % RING]
         return remote(part, part, out_c.at[turn(item)], in_c.at[turn(item)], (me, rank))
 
     def add_to(item, index, where, source):
@@ -344,7 +342,7 @@
         repeat(
             pairs,
             lambda step: add_to(
-                item, step, pl.ds(0, full), from_core.at[lax.rem(turn(item), RING), step]
+                item, step, pl.ds(0, full), from_core.at[turn(item) % RING, step]
             ),
         )
 
@@ -415,7 +413,7 @@
         return total
 
     def unit_place(item, which):
-        return 4 + 2 * (which * (parts // 2) + lax.div(item, 2)) + lax.rem(item, 2)
+        return 4 + 2 * (which * (parts // 2) + item // 2) + item % 2
 
     def side_copy(item):
         return remote(
@@ -626,8 +624,10 @@
             branch[part] = (gate * grad_rows[part].astype(F32)).astype(BF16)
 
         by_rows(body)
+        transpose_to(branch_t, branch)
+
+    def send_branch():
         branch_copy().start()
-        transpose_to(branch_t, branch)
 
     def project(which):
         def body(part):
@@ -682,10 +682,7 @@
         repeat(2 * blocks, lambda i: body(span(lax.rem(i, 2), count), span(lax.div(i, 2), block)))
 
     def go_up(up):
-        @pl.when(up == 4)
-        def _():
-            branch_copy().wait_recv()
-            transpose_to(branch_t, branch, count)
+        if up == 4:
             norm_copy().wait_recv()
             transpose_to(norm_two_t, norm_two, count)
 
@@ -698,6 +695,10 @@
         by_lines(units_of)
 
     def go_down(up, down):
+        if up == 4:
+            branch_copy().wait_recv()
+            transpose_to(branch_t, branch, count)
+
         def units_of(lines, part):
             grad_hidden = contract(branch[lines], held[down, :, part], 1, 0)
             grad_pre[lines, part] = (grad_hidden * slopes[lines, part]).astype(BF16)
@@ -711,8 +712,8 @@
             by_blocks(body)
 
         def pass_on(source, target, copy):
-            @pl.when(down == chunks - 1)
-            def _():
+            if down == chunks - 1:
+
                 def body(part):
                     target[part] = source[pl.ds(part.start + count, tile)].astype(BF16)
 
@@ -767,7 +768,19 @@
             held[3, :, part] = contract(grad_attended_t[...], context[:, part], 1, 0).astype(BF16)
 
         by_blocks(weights)
-        give_core(jnp.int32(units + PAUSE))
+
+    def recall():
+        def body(index):
+            part = span(index, 2 * HD)
+            for seq in range(seqs):
+                place = pl.ds(seq * caps, caps)
+                queries, keys = qkv[0, place, part], qkv[1, place, part]
+                for head in range(2):
+                    slopes[pl.ds((2 * seq + head) * caps, caps), part] = probabilities(
+                        seq, queries, keys, head
+                    )
+
+        repeat(full // (2 * HD), body)
 
     def attend_back():
         def body(index):
@@ -778,7 +791,7 @@
                 values, grad = qkv[2, place, part], grad_context[place, part]
                 grad_q, grad_k, grad_v = 0.0, 0.0, 0.0
                 for head in range(2):
-                    probs = probabilities(seq, queries, keys, head)
+                    probs = slopes[pl.ds((2 * seq + head) * caps, caps), part]
                     grad_probs = contract(own_lanes(grad, head), values, 1, 1)
                     inner = jnp.sum(probs * grad_probs, axis=-1, keepdims=True)
                     grad_scores = (probs * (grad_probs - inner)).astype(BF16)
@@ -801,6 +814,8 @@
             grad_one[:, part] = total
 
         by_blocks(through)
+
+    def weigh_back():
         transpose_to(norm_one_t, norm_one)
 
         def weights(part):
@@ -810,8 +825,6 @@
                 )
 
         by_blocks(weights)
-        for item in range(units + PAUSE + 1, units + PAUSE + 4):
-            give_core(jnp.int32(item))
 
     def close():
         mlp_copy().wait_recv()
@@ -864,65 +877,81 @@
     keep_vec.wait()
     vec_gather(0)
 
-    lead = AHEAD * bits
-    first = lead + 5
-    items = chunks + PAUSE
-    vec_first = lead + chunks + 6
-
-    def tick(now, _):
-        for stage in range(bits, -1, -1):
-            chunk = now - AHEAD * stage
-
-            @pl.when((chunk >= 0) & (chunk < chunks))
-            def _(chunk=chunk, stage=stage):
-                pl.when(chunk < 4)(lambda: gather_stage(chunk, 0, stage))
-                pl.when(chunk >= 4)(lambda: gather_stage(chunk, 1, stage))
-
-        for stage in range(1, bits + 1):
-            pl.when(now == stage)(functools.partial(vec_gather, stage))
-
-        @pl.when(now == 1)
-        def _():
-            for chunk in range(4, chunks):
-                start_z(chunk)
-
-        for seq in range(seqs):
-            for which, target in enumerate((picked, grad_rows)):
-                order = 2 * seq + which
-                place = (which * seqs + seq) * halves
-                pl.when(now == order)(functools.partial(pick, target, seq, place))
-            pl.when(now == 2 * seq)(functools.partial(mask, seq))
-
-        @pl.when(now == max(bits, 2 * seqs - 1) + 1)
-        def _():
-            spell_params()
-            prepare()
-
-        whole = now - lead
-        pl.when((whole >= 0) & (whole < 3))(lambda: project(whole))
-        pl.when(whole == 2)(attend)
-        pl.when(whole == 3)(leave_attention)
-        units_in = (whole >= 4) & (whole < chunks)
-        pl.when(units_in & (lax.rem(whole, 2) == 0))(lambda: go_up(whole))
-        pl.when(units_in & (lax.rem(whole, 2) == 1))(lambda: go_down(whole - 1, whole))
-        for stage in range(bits + 1, -1, -1):
-            item = now - first - AHEAD * stage
-            inside = (item >= 0) & (item < items)
-            pl.when(inside & (item < units))(functools.partial(scatter_stage, item, 1, stage))
-            if stage > 0:
-                late = inside & (item >= units + PAUSE)
-                pl.when(late)(functools.partial(scatter_stage, item, 0, stage))
-
-        pl.when(whole == chunks + 1)(enter_back)
-        pl.when(whole == chunks + 2)(attend_back)
-        pl.when(whole == chunks + 3)(leave_back)
-        pl.when(whole == chunks + 5)(close)
-        for stage in range(bits + 1):
-            pl.when(now == vec_first + AHEAD * stage)(functools.partial(vec_stage, stage))
-        pl.when(now == vec_first + AHEAD * (bits + 1))(vec_finish)
-
-    last = max(first + items - 1 + AHEAD * (bits + 1), vec_first + AHEAD * (bits + 1))
-    lax.fori_loop(0, last + 1, tick, None)
+    events = []
+
+    def at(when, what, *args):
+        events.append((when, len(events), functools.partial(what, *args)))
+
+    def between(first, last, step, steps):
+        return first + (last - first) * step / max(steps, 1)
+
+    for stage in range(1, bits + 1):
+        at(3.8 + 2.2 * stage, vec_gather, stage)
+    for seq in range(seqs):
+        at(9 + seq, mask, seq)
+        for which, target in enumerate((picked, grad_rows)):
+            at(9 + seq, pick, target, seq, (which * seqs + seq) * halves)
+    for chunk in range(4, chunks):
+        at(7.5, start_z, chunk)
+    at(3.8 + 2.2 * bits + 3.2, spell_params)
+    at(3.8 + 2.2 * bits + 3.2, prepare)
+    weights_in = [33 + 8.5 * chunk for chunk in range(4)] + [
+        71 + 11.2 * chunk for chunk in range(units)
+    ]
+    for chunk in range(chunks):
+        kind = int(chunk >= 4)
+        opened = (54 + 8.3 * (chunk - 4)) if kind else (13 + 8.5 * chunk)
+        for stage in range(kind, bits):
+            when = between(opened, weights_in[chunk] - 4, stage - kind, bits - 1 - kind)
+            at(when, gather_stage, chunk, kind, stage)
+        at(weights_in[chunk], gather_stage, chunk, kind, bits)
+    for chunk in range(3):
+        at(weights_in[chunk], project, chunk)
+    at(47, send_branch)
+    at(weights_in[2], attend)
+    at(weights_in[3], leave_attention)
+    for item in range(0, units, 2):
+        up, down = item + 4, item + 5
+        at(max(weights_in[up], 74) + 0.1, go_up, up)
+        ready = weights_in[down] + 0.1
+        at(ready, go_down, up, down)
+        for one in (item, item + 1):
+            at(ready, give_core, one)
+    at(116.5, recall)
+    at(120, enter_back)
+    at(120, give_core, units)
+    at(126, attend_back)
+    at(134, leave_back)
+    at(134, close)
+    at(134.2, weigh_back)
+    for item in range(units + 1, chunks):
+        at(134.3, give_core, item)
+    summed = [
+        (93.1, 115, 116, 147, 178),
+        (93.1, 123, 124, 147.1, 178),
+        (115, 132, 133, 148, 178),
+        (115.1, 145, 146, 172, 184),
+        (125, 152, 163, 170, 0),
+        (143, 158, 168, 175, 0),
+        (143.2, 164, 174, 181, 0),
+        (143.3, 170, 180, 187, 0),
+    ]
+    for item, (core_in, second, last, across, aside) in enumerate(summed):
+        kind = int(item < units)
+        final = bits - kind
+        at(core_in, scatter_stage, item, kind, 1)
+        for stage in range(2, final + 1):
+            when = last if final == 2 else between(second, last, stage - 2, final - 2)
+            at(when, scatter_stage, item, kind, stage)
+        at(across, scatter_stage, item, kind, final + 1)
+        if kind:
+            at(aside, scatter_stage, item, kind, final + 2)
+    for stage in range(bits + 1):
+        when = (134.1, 142.9, 143.1, 164.5)[stage] if stage < 4 else 164.5 + 2 * stage
+        at(when, vec_stage, stage)
+    at(188, vec_finish)
+    for _, _, event in sorted(events, key=lambda event: event[:2]):
+        event()
 
     branch_copy().wait_send()
     norm_copy().wait_send()
@@ -938,8 +967,8 @@
         if kind:
             side_copy(item).wait_send()
 
-    repeat(units, lambda item: drain(item, 1))
-    repeat(4, lambda item: drain(item + units + PAUSE, 0))
+    for item in range(chunks):
+        drain(item, int(item < units))
 
 
 def run_layer(bits, ranks, shards, vec, routes, pic_start, activations, cotangent):

time: 240 us -> 223 us (0.929)
  Pallas kernels: 233 us -> 216 us
    pallas_call x1, Pallas kernels: 223 us -> 206 us  [run_layer(): pl.pallas_call(functools.partial(layer_kernel, bits, ranks, chunks, parts...]
where the time goes in v5:
time: 223 us; the launch traced here: 222 us
  Pallas kernels  216 us (97%)
  local copies, waits for them, and re-layouts  3.6 us (2%)
  other arithmetic  2.38 us (1%)
    pallas_call x1, Pallas kernels, run_layer(): pl.pallas_call(functools.partial(layer_kernel, bits, ranks, chunks, parts...  206 us
    pallas_call x1, Pallas kernels, put_rows(): pl.pallas_call(functools.partial(put_kernel, seqs, steps), grid=(seqs * s...  10 us

profile of v5, /device:TPU:0, one launch (start us, length us, event | category | flops | bytes accessed | tf_op | source)
XLA Modules:
  0.0 222.4 jit_solution(5286629531071494622)
XLA Ops:
  0.6 1.3 fusion.5.refs_6_
  1.9 205.8 %layer_kernel.1 = (f32[12,128,256]{2,1,0:T(8,128)}, f32[8,128]{1,0:T(8,128)}, bf16[256,1024]{1,0:T(8,128)(2,1)}, bf16[256,1024]{1,0:T(8,128)(2,1)}) custom-call(bf16[128,256]{1,0:T(8,128)(2,1)} %refs_0_.1, bf16[128,256]{1,0:T(8,128)(2,1)} %refs_1_.1, bf16[128,256]{1,0:T(8,128)(2,1)} %refs_2_.1, bf16[128,256]{1,0:T(8,128)(2,1)} %refs_3_.1, ...), custom_call_target="tpu_custom_call" | custom-call | tf_op jit(solution)/shard_map/layer_kernel/pallas_call | solution.py:989
  207.7 1.3 slice_bitcast_fusion.12
  209.1 2.3 %slice_bitcast_fusion.3 = (f32[128,256]{1,0:T(8,128)S(1)}, f32[128,256]{1,0:T(8,128)S(1)}, f32[128,256]{1,0:T(8,128)S(1)}, f32[128,256]{1,0:T(8,128)S(1)}, f32[1...) fusion(f32[12,128,256]{2,1,0:T(8,128)} %get-tuple-element.22), kind=kLoop, calls=%fused_computation.5 | loop fusion | bytes 3145728 | tf_op jit(solution)/shard_map/squeeze | solution.py:1135
  211.3 1.1 pad_maximum_fusion
  212.4 10.0 %put_rows.1 = (bf16[2,1024,1024]{2,1,0:T(8,128)(2,1)}, bf16[2,1024,1024]{2,1,0:T(8,128)(2,1)}) custom-call(s32[8,128]{1,0:T(8,128)} %routes.1, bf16[256,1024]{1,0:T(8,128)(2,1)} %get-tuple-element.17.new_rows, bf16[256,1024]{1,0:T(8,128)(2,1)} %get-tuple-element.18.new_grads, bf16[2,1024,1024]{2,1,0:T(8,128)(2,1)} %activations.1, ...), custom_call_target="tpu_custom_call" | custom-call | tf_op jit(solution)/shard_map/put_rows/pallas_call | solution.py:1097

commit v6 on v5

--- a/solution.py
+++ b/solution.py
@@ -930,11 +930,11 @@
         (93.1, 115, 116, 147, 178),
         (93.1, 123, 124, 147.1, 178),
         (115, 132, 133, 148, 178),
-        (115.1, 145, 146, 172, 184),
-        (125, 152, 163, 170, 0),
-        (143, 158, 168, 175, 0),
-        (143.2, 164, 174, 181, 0),
-        (143.3, 170, 180, 187, 0),
+        (115.1, 143.1, 143.15, 173, 184),
+        (125, 143.2, 160, 177, 0),
+        (143, 158, 170, 181, 0),
+        (143.3, 166, 175, 185, 0),
+        (158.1, 172, 178, 187, 0),
     ]
     for item, (core_in, second, last, across, aside) in enumerate(summed):
         kind = int(item < units)
@@ -947,7 +947,7 @@
         if kind:
             at(aside, scatter_stage, item, kind, final + 2)
     for stage in range(bits + 1):
-        when = (134.1, 142.9, 143.1, 164.5)[stage] if stage < 4 else 164.5 + 2 * stage
+        when = (134.1, 142.9, 143.05, 164.5)[stage] if stage < 4 else 164.5 + 2 * stage
         at(when, vec_stage, stage)
     at(188, vec_finish)
     for _, _, event in sorted(events, key=lambda event: event[:2]):

time: 223 us -> 215 us (0.964)
  Pallas kernels: 216 us -> 208 us
    pallas_call x1, Pallas kernels: 206 us -> 198 us  [run_layer(): pl.pallas_call(functools.partial(layer_kernel, bits, ranks, chunks, parts...]
where the time goes in v6:
time: 215 us
  Pallas kernels  208 us (97%)
  local copies, waits for them, and re-layouts  3.6 us (2%)
  other arithmetic  2.38 us (1%)
    pallas_call x1, Pallas kernels, run_layer(): pl.pallas_call(functools.partial(layer_kernel, bits, ranks, chunks, parts...  198 us
    pallas_call x1, Pallas kernels, put_rows(): pl.pallas_call(functools.partial(put_kernel, seqs, steps), grid=(seqs * s...  10 us

profile of v6, /device:TPU:0, one launch (start us, length us, event | category | flops | bytes accessed | tf_op | source)
XLA Modules:
  0.0 214.9 jit_solution(5356804827097251491)
XLA Ops:
  0.6 1.3 fusion.5.refs_6_
  1.9 198.2 %layer_kernel.1 = (f32[12,128,256]{2,1,0:T(8,128)}, f32[8,128]{1,0:T(8,128)}, bf16[256,1024]{1,0:T(8,128)(2,1)}, bf16[256,1024]{1,0:T(8,128)(2,1)}) custom-call(bf16[128,256]{1,0:T(8,128)(2,1)} %refs_0_.1, bf16[128,256]{1,0:T(8,128)(2,1)} %refs_1_.1, bf16[128,256]{1,0:T(8,128)(2,1)} %refs_2_.1, bf16[128,256]{1,0:T(8,128)(2,1)} %refs_3_.1, ...), custom_call_target="tpu_custom_call" | custom-call | tf_op jit(solution)/shard_map/layer_kernel/pallas_call | solution.py:989
  200.2 1.3 slice_bitcast_fusion.12
  201.5 2.3 %slice_bitcast_fusion.3 = (f32[128,256]{1,0:T(8,128)S(1)}, f32[128,256]{1,0:T(8,128)S(1)}, f32[128,256]{1,0:T(8,128)S(1)}, f32[128,256]{1,0:T(8,128)S(1)}, f32[1...) fusion(f32[12,128,256]{2,1,0:T(8,128)} %get-tuple-element.22), kind=kLoop, calls=%fused_computation.5 | loop fusion | bytes 3145728 | tf_op jit(solution)/shard_map/squeeze | solution.py:1135
  203.8 1.1 pad_maximum_fusion
  204.8 10.0 %put_rows.1 = (bf16[2,1024,1024]{2,1,0:T(8,128)(2,1)}, bf16[2,1024,1024]{2,1,0:T(8,128)(2,1)}) custom-call(s32[8,128]{1,0:T(8,128)} %routes.1, bf16[256,1024]{1,0:T(8,128)(2,1)} %get-tuple-element.17.new_rows, bf16[256,1024]{1,0:T(8,128)(2,1)} %get-tuple-element.18.new_grads, bf16[2,1024,1024]{2,1,0:T(8,128)(2,1)} %activations.1, ...), custom_call_target="tpu_custom_call" | custom-call | tf_op jit(solution)/shard_map/put_rows/pallas_call | solution.py:1097

commit v7 on v6

--- a/solution.py
+++ b/solution.py
@@ -95,7 +95,12 @@
     pic_start,
     activations,
     cotangent,
-    sums,
+    sum_query,
+    sum_key,
+    sum_value,
+    sum_proj,
+    sum_up,
+    sum_down,
     vec_sum,
     new_rows,
     new_grads,
@@ -412,8 +417,9 @@
             total = total + from_z[turn(item), (hop - 1) * (1 + kind) + which].astype(F32)
         return total
 
-    def unit_place(item, which):
-        return 4 + 2 * (which * (parts // 2) + item // 2) + item % 2
+    def put_units(item, which, values):
+        place = span(which * (parts // 2) + item // 2, width)
+        (sum_up, sum_down)[item % 2][:, place] = values
 
     def side_copy(item):
         return remote(
@@ -433,12 +439,13 @@
             if kind:
                 side_out[item] = total_of(item, kind, 1).astype(BF16)
                 side_copy(item).start()
-                sums[unit_place(item, side)] = total_of(item, kind, 0)
+                put_units(item, side, total_of(item, kind, 0))
             else:
-                sums[slot(item)] = total_of(item, kind, 0)
+                out = (sum_query, sum_key, sum_value, sum_proj)[slot(item)]
+                out[...] = total_of(item, kind, 0)
         elif stage == bits - kind + 2:
             side_copy(item).wait_recv()
-            sums[unit_place(item, 1 - side)] = side_in[item].astype(F32)
+            put_units(item, 1 - side, side_in[item].astype(F32))
         if stage == 0:
             give_core(item)
         elif stage < bits - kind:
@@ -989,13 +996,14 @@
     return pl.pallas_call(
         functools.partial(layer_kernel, bits, ranks, chunks, parts),
         out_shape=[
-            jax.ShapeDtypeStruct((4 + 2 * parts, rows, width), F32),
+            *[jax.ShapeDtypeStruct((rows, width), F32)] * 4,
+            *[jax.ShapeDtypeStruct((rows, width * parts), F32)] * 2,
             jax.ShapeDtypeStruct((8, 128), F32),
             jax.ShapeDtypeStruct((count, full), BF16),
             jax.ShapeDtypeStruct((count, full), BF16),
         ],
         in_specs=[ANY] * 6 + [VMEM] * 2 + [pl.BlockSpec(memory_space=pltpu.SMEM)] + [ANY] * 2,
-        out_specs=[VMEM] * 4,
+        out_specs=[VMEM] * 9,
         scratch_shapes=[
             low,
             low,
@@ -1070,40 +1078,6 @@
     )(*shards, vec, routes, pic_start, activations, cotangent)
 
 
-def put_kernel(seqs, steps, routes, new_rows, new_grads, activations, cotangent, result, grad_input):
-    index = pl.program_id(0)
-    seq, step = lax.div(index, steps), lax.rem(index, steps)
-    size, caps = activations.shape[1], routes.shape[1]
-    place = routes[pl.ds(lax.axis_index("tensor") * seqs + seq, 1), :]
-    line = lax.broadcasted_iota(jnp.int32, (size, caps), 0) + step * size
-    chosen = (line == place).astype(F32)
-    routed = jnp.max(chosen, axis=-1, keepdims=True) > 0
-    chosen = chosen.astype(BF16)
-    for new, base, out in (
-        (new_rows, activations, result),
-        (new_grads, cotangent, grad_input),
-    ):
-        placed = contract(chosen, new[...], 1, 0)
-        out[0] = jnp.where(routed, placed, base[0].astype(F32)).astype(BF16)
-
-
-def put_rows(routes, new_rows, new_grads, activations, cotangent):
-    seqs, length, full = activations.shape
-    caps = routes.shape[1]
-    steps = 4
-    size = length // steps
-    large = pl.BlockSpec((1, size, full), lambda index: (index // steps, index % steps, 0))
-    small = pl.BlockSpec((caps, full), lambda index: (index // steps, 0))
-    return pl.pallas_call(
-        functools.partial(put_kernel, seqs, steps),
-        grid=(seqs * steps,),
-        out_shape=[jax.ShapeDtypeStruct(activations.shape, BF16)] * 2,
-        in_specs=[pl.BlockSpec(routes.shape, lambda index: (0, 0)), small, small, large, large],
-        out_specs=[large, large],
-        name="put_rows",
-    )(routes, new_rows, new_grads, activations, cotangent)
-
-
 def shards(
     activations,
     routes,
@@ -1126,26 +1100,30 @@
     vec = jnp.stack([router_w, gain_attn, gain_mlp]).astype(F32)
     vec = jnp.pad(vec, ((0, 5), (0, 128 - rows)))
     weights = (w_query, w_key, w_value, w_proj, w_up, w_down)
-    sums, small, new_rows, new_grads = run_layer(
+    *sums, small, new_rows, new_grads = run_layer(
         bits, ranks, weights, vec, routes, pic_start, activations, cotangent
     )
-    result, grad_input = put_rows(routes, new_rows, new_grads, activations, cotangent)
-
-    def side_by_side(first):
-        return jnp.concatenate([sums[first + 2 * part] for part in range(parts)], axis=1)
+    seqs, length, features = activations.shape
+    own = lax.dynamic_slice_in_dim(routes, lax.axis_index("tensor") * seqs, seqs, 0)
+    chosen = (own[:, :, None] == jnp.arange(length)[None, None, :]).astype(BF16)
+    routed = jnp.sum(chosen.astype(F32), axis=1) > 0
+
+    def put(base, new):
+        placed = jnp.einsum(
+            "scl,scd->sld",
+            chosen,
+            new.reshape(seqs, -1, features),
+            preferred_element_type=F32,
+        )
+        return jnp.where(routed[:, :, None], placed.astype(BF16), base)
 
     return (
-        result,
-        grad_input,
+        put(activations, new_rows),
+        put(cotangent, new_grads),
         small[3, :rows],
         small[4, :rows],
         small[5, :rows],
-        sums[0],
-        sums[1],
-        sums[2],
-        sums[3],
-        side_by_side(4),
-        side_by_side(5),
+        *sums,
     )
 
 

time: 215 us -> 215 us (level)
  Pallas kernels: 208 us -> 198 us
  matrix products: 0 us -> 7.42 us
  local copies, waits for them, and re-layouts: 3.6 us -> 6.26 us
    pallas_call x1 -> x0, Pallas kernels: 10 us -> none  [put_rows(): pl.pallas_call(functools.partial(put_kernel, seqs, steps), grid=(seqs * s...]
    dot_general x0 -> x2, matrix products: none -> 7.42 us  [put(): jnp.einsum('scl,scd->sld', chosen, new.reshape(seqs, -1, features), prefe...]
    unnamed x0 -> x28, local copies, waits for them, and re-layouts: none -> 4.25 us
    squeeze x1 -> x0, local copies, waits for them, and re-layouts: 2.29 us -> none  [side_by_side(): sums[first + 2 * part]]
where the time goes in v7:
time: 215 us
  Pallas kernels  198 us (92%)
  matrix products  7.42 us (3%)
  local copies, waits for them, and re-layouts  6.26 us (3%)
    pallas_call x1, Pallas kernels, run_layer(): pl.pallas_call(functools.partial(layer_kernel, bits, ranks, chunks, parts...  198 us
    dot_general x2, matrix products, put(): jnp.einsum('scl,scd->sld', chosen, new.reshape(seqs, -1, features), prefe...  7.42 us

profile of v7, /device:TPU:0, one launch (start us, length us, event | category | flops | bytes accessed | tf_op | source)
XLA Modules:
  0.0 214.7 jit_solution(250258246666481260)
XLA Ops:
  0.6 0.7 constant_dynamic-slice_fusion
  1.3 0.0 copy-start.9
  1.3 1.3 fusion.8.refs_6_
  2.6 0.0 copy-done.9
  2.6 0.2 convert_reduce_fusion
  2.9 0.6 broadcast_compare_fusion
  3.5 198.1 %layer_kernel.1 = (f32[128,256]{1,0:T(8,128)}, f32[128,256]{1,0:T(8,128)}, f32[128,256]{1,0:T(8,128)}, f32[128,256]{1,0:T(8,128)}, f32[128,1024]{1,0:T(8,128)}, ...) custom-call(bf16[128,256]{1,0:T(8,128)(2,1)} %refs_0_.1, ...), custom_call_target="tpu_custom_call" | custom-call | tf_op jit(solution)/shard_map/layer_kernel/pallas_call | solution.py:996
  201.6 1.3 slice_bitcast_fusion
  202.9 0.0 copy-start
  202.9 0.0 copy-start.1
  202.9 0.0 copy-start.8
  202.9 0.0 copy-start.10
  202.9 4.6 %convert_select_fusion = bf16[2,1024,1024]{2,1,0:T(8,128)(2,1)} fusion(bf16[2,1024,1024]{2,1,0:T(8,128)(2,1)} %refs_10_.1, pred[2,1024]{1,0:T(4,128)(4,1)} %broadcast_compare_fusion, bf16[2,128,1024]{2,1,0:T(8,128)(2,1)} %bitcast.14, s32[2,128]{1,0:T(2,128)} %copy-done.9), kind=kOutput, calls=%fused_computation | convolution fusion | flops 541327360 | bytes 8915968 | tf_op jit(solution)/shard_map/scl,scd->sld/dot_general | solution.py:1112
  207.6 0.0 copy-done
  207.6 0.0 copy-done.1
  207.6 0.0 copy-done.8
  207.6 0.0 copy-done.10
  207.6 0.0 copy-start.7
  207.6 0.0 copy-start.6
  207.6 0.0 copy-start.5
  207.6 0.0 copy-start.4
  207.6 0.0 copy-start.3
  207.6 0.0 copy-start.2
  207.7 2.8 %convert_select_fusion.1 = bf16[2,1024,1024]{2,1,0:T(8,128)(2,1)} fusion(bf16[2,1024,1024]{2,1,0:T(8,128)(2,1)S(1)} %copy-done, pred[2,1024]{1,0:T(4,128)(4,1)S(1)} %copy-done.8, bf16[2,128,1024]{2,1,0:T(8,128)(2,1)S(1)} %bitcast.13, s32[2,128]{1,0:T(2,128)S(1)} %copy-done.10), kind=kOutput, calls=%fused_computation.1 | convolution fusion | flops 541327360 | bytes 8915968 | tf_op jit(solution)/shard_map/scl,scd->sld/dot_general | solution.py:1112
  210.4 0.0 copy-done.7
  210.4 0.7 copy.30
  211.1 0.0 copy-done.6
  211.1 0.7 copy.31
  211.8 0.0 copy-done.5
  211.8 0.7 copy.32
  212.4 0.0 copy-done.4
  212.4 0.7 copy.33
  213.1 0.0 copy-done.3
  213.1 0.8 copy.34
  213.9 0.0 copy-done.2
  213.9 0.8 copy.35
Async XLA Ops:
  1.3 1.3 copy-start.9
  202.9 4.7 %copy-start = (bf16[2,1024,1024]{2,1,0:T(8,128)(2,1)S(1)}, bf16[2,1024,1024]{2,1,0:T(8,128)(2,1)}, u32[]{:S(2)}) copy-start(bf16[2,1024,1024]{2,1,0:T(8,128)(2,1)} %refs_9_.1) | copy-start | bytes 12582916
  202.9 4.7 %copy-start.1 = (bf16[256,1024]{1,0:T(8,128)(2,1)S(1)}, bf16[256,1024]{1,0:T(8,128)(2,1)}, u32[]{:S(2)}) copy-start(bf16[256,1024]{1,0:T(8,128)(2,1)} %get-tuple-element.20) | copy-start | bytes 1572868
  202.9 4.7 %copy-start.8 = (pred[2,1024]{1,0:T(4,128)(4,1)S(1)}, pred[2,1024]{1,0:T(4,128)(4,1)}, u32[]{:S(2)}) copy-start(pred[2,1024]{1,0:T(4,128)(4,1)} %broadcast_compare_fusion) | copy-start | bytes 6148
  202.9 4.7 %copy-start.10 = (s32[2,128]{1,0:T(2,128)S(1)}, s32[2,128]{1,0:T(2,128)}, u32[]{:S(2)}) copy-start(s32[2,128]{1,0:T(2,128)} %copy-done.9) | copy-start | bytes 3076
  207.6 2.8 %copy-start.7 = (f32[128,256]{1,0:T(8,128)S(1)}, f32[128,256]{1,0:T(8,128)}, u32[]{:S(2)}) copy-start(f32[128,256]{1,0:T(8,128)} %get-tuple-element.48) | copy-start | bytes 393220
  207.6 3.5 %copy-start.6 = (f32[128,256]{1,0:T(8,128)S(1)}, f32[128,256]{1,0:T(8,128)}, u32[]{:S(2)}) copy-start(f32[128,256]{1,0:T(8,128)} %get-tuple-element.49) | copy-start | bytes 393220
  207.6 4.1 %copy-start.5 = (f32[128,256]{1,0:T(8,128)S(1)}, f32[128,256]{1,0:T(8,128)}, u32[]{:S(2)}) copy-start(f32[128,256]{1,0:T(8,128)} %get-tuple-element.50) | copy-start | bytes 393220
  207.6 4.8 %copy-start.4 = (f32[128,256]{1,0:T(8,128)S(1)}, f32[128,256]{1,0:T(8,128)}, u32[]{:S(2)}) copy-start(f32[128,256]{1,0:T(8,128)} %get-tuple-element.51) | copy-start | bytes 393220
  207.6 5.4 %copy-start.3 = (f32[128,1024]{1,0:T(8,128)S(1)}, f32[128,1024]{1,0:T(8,128)}, u32[]{:S(2)}) copy-start(f32[128,1024]{1,0:T(8,128)} %get-tuple-element.52) | copy-start | bytes 1572868
  207.6 6.2 %copy-start.2 = (f32[128,1024]{1,0:T(8,128)S(1)}, f32[128,1024]{1,0:T(8,128)}, u32[]{:S(2)}) copy-start(f32[128,1024]{1,0:T(8,128)} %get-tuple-element.53) | copy-start | bytes 1572868
